TPU v7x, 32 devices: a whole 2x2x4 slice. The times are simulated.
32 devices in a mesh: seq: 8 (over z, x), head: 4 (over y, core).
Axes of the slice: x: 2, y: 2, z: 4, core: 2. Of those that a mesh axis runs over, the one named last changes fastest.
Arguments:
- q_latent: bfloat16 [2048, 1536], P('seq', 'head'), may hold values from -6 to 6
- kv_latent: bfloat16 [2048, 512], P('seq', 'head'), may hold values from -6 to 6
- k_rope: bfloat16 [2048, 64], P('seq'), may hold values from -6 to 6
- segment_ids: int32 [2048], P('seq'), may hold values from 0 to 7, as said below
- w_q_nope: bfloat16 [1536, 16384], P('seq', 'head'), may hold values from -6 to 6
- w_q_rope: bfloat16 [1536, 8192], P('seq', 'head'), may hold values from -6 to 6
- w_kv_nope: bfloat16 [512, 16384], P('seq', 'head'), may hold values from -6 to 6
- threshold: float32 [1], replicated, may hold values from 3.5 to 5.5
Outputs:
- new_q_nope: bfloat16 [1536, 16384], P('seq', 'head')
- new_q_rope: bfloat16 [1536, 8192], P('seq', 'head')
- new_kv_nope: bfloat16 [512, 16384], P('seq', 'head')
- head_max: float32 [128], P('head')
- row_max: float32 [2048, 128], P('seq', 'head')
Inputs may be any that keep to these rules, and one draw needn't show every extreme that they name: segment_ids never fall along the tokens and each document has 1 to 768 tokens.
All inputs are finite; a program needn't handle non-finite values.
Results may differ from a plain program's by a relative error of at most 0.0034.
Values may be sent and summed in bfloat16 or wider, within the bound.
A program may use at most 128 MiB of HBM per device.

v0:
```python
import functools
import math

import jax
import jax.numpy as jnp
from jax import lax
from jax.experimental import pallas as pl
from jax.experimental.pallas import tpu as pltpu
from jax.sharding import PartitionSpec as P

D_NOPE = 128
D_ROPE = 64
QLORA = 1536
KVLORA = 512
REACH = 3


def as_sent(value):
    return jax.tree.map(lambda a: a.astype(jnp.bfloat16) if a.dtype == jnp.float32 else a, value)


def from_partner(value, axis, stride):
    mask = 2**stride
    pairs = [(source, source ^ mask) for source in range(lax.axis_size(axis))]
    return lax.ppermute(value, axis, pairs)


def shifted(block, axis, distance):
    devices = range(lax.axis_size(axis))
    route = [(i - distance, i) for i in devices if i - distance in devices]
    return lax.ppermute(block, axis, route)


def score_max(query_nope, query_rope, key_nope, key_rope, allowed):
    nope = jnp.einsum("qhd,khd->hqk", query_nope, key_nope, preferred_element_type=jnp.float32)
    rope = jnp.einsum("qhd,kd->hqk", query_rope, key_rope, preferred_element_type=jnp.float32)
    scores = (nope + rope) * (1.0 / math.sqrt(D_NOPE + D_ROPE))
    return jnp.max(jnp.where(allowed[None], scores, jnp.float32(-1e30)), axis=2)


def masked_max(compute, operands):
    return compute(*operands)


def spread_columns(weight, width, quarter, copies):
    pieces = weight.reshape(weight.shape[0], 4, quarter * width).transpose(1, 0, 2)
    return jnp.tile(pieces, (copies, 1, 1))


def grouped_body(q_latent, kv_latent, k_rope, segment_ids, w_q_nope, w_q_rope, w_kv_nope, threshold):
    q_whole, kv_whole = (
        lax.all_gather(q_latent, "head", axis=1, tiled=True),
        lax.all_gather(kv_latent, "head", axis=1, tiled=True),
    )
    rows = q_whole.shape[0]
    heads = w_q_nope.shape[1] // D_NOPE
    q_scale = 1.0 / math.sqrt(QLORA)
    k_scale = 1.0 / math.sqrt(KVLORA)
    place = lax.axis_index("seq")
    quarter = heads // 4
    copies = lax.axis_size("seq") // 4
    slot = place % 4
    sent = (
        spread_columns(w_q_nope, D_NOPE, quarter, copies),
        spread_columns(w_q_rope, D_ROPE, quarter, copies),
        spread_columns(w_kv_nope, D_NOPE, quarter, copies),
    )
    got_nope, got_rope, got_kv = (
        lax.all_to_all(sent[0], "seq", split_axis=0, concat_axis=1, tiled=True),
        lax.all_to_all(sent[1], "seq", split_axis=0, concat_axis=1, tiled=True),
        lax.all_to_all(sent[2], "seq", split_axis=0, concat_axis=1, tiled=True),
    )
    sub_nope = got_nope.reshape(QLORA, quarter * D_NOPE)
    sub_rope = got_rope.reshape(QLORA, quarter * D_ROPE)
    sub_kv = got_kv.reshape(KVLORA, quarter * D_NOPE)
    group = (q_whole, kv_whole, k_rope)
    for level in range(2):
        partner = jax.tree.map(
            lambda part, own: part.astype(own.dtype),
            from_partner(as_sent(group), "seq", level),
            group,
        )
        upper = place // (1 << level) % 2 == 1
        group = tuple(
            (
                jnp.where(
                    upper, jnp.concatenate([other, mine], 0), jnp.concatenate([mine, other], 0)
                )
                for mine, other in zip(group, partner)
            )
        )
    group_q, group_kv, group_rope = group
    early_kv, early_rope = shifted(
        (group_kv[(4 - REACH) * rows :], group_rope[(4 - REACH) * rows :]), "seq", 4
    )
    keys_kv = jnp.concatenate([early_kv, group_kv], 0)
    keys_rope = jnp.concatenate([early_rope, group_rope], 0)
    key_nope = (
        (jnp.dot(keys_kv, sub_kv, preferred_element_type=jnp.float32) * k_scale)
        .astype(jnp.bfloat16)
        .reshape(keys_kv.shape[0], quarter, D_NOPE)
    )
    query_nope = (
        (jnp.dot(group_q, sub_nope, preferred_element_type=jnp.float32) * q_scale)
        .astype(jnp.bfloat16)
        .reshape(4 * rows, quarter, D_NOPE)
    )
    query_rope = (
        (jnp.dot(group_q, sub_rope, preferred_element_type=jnp.float32) * q_scale)
        .astype(jnp.bfloat16)
        .reshape(4 * rows, quarter, D_ROPE)
    )
    all_segs = lax.all_gather(segment_ids, "seq", axis=0, tiled=True)
    padded_segs = jnp.concatenate([jnp.full((REACH * rows,), -1, jnp.int32), all_segs], 0)
    first = place // 4 * 4
    window = (REACH + 1) * rows
    block_rows = []
    for local in range(4):
        block = first + local
        query_seg = lax.dynamic_slice_in_dim(all_segs, block * rows, rows, 0)
        key_seg = lax.dynamic_slice_in_dim(padded_segs, block * rows, window, 0)
        query_pos = block * rows + jnp.arange(rows, dtype=jnp.int32)
        key_pos = (block - REACH) * rows + jnp.arange(window, dtype=jnp.int32)
        allowed = (
            (query_seg[:, None] == key_seg[None, :])
            & (key_pos[None, :] <= query_pos[:, None])
            & (key_pos[None, :] >= 0)
        )
        operands = (
            query_nope[local * rows : (local + 1) * rows],
            query_rope[local * rows : (local + 1) * rows],
            key_nope[local * rows : local * rows + window],
            keys_rope[local * rows : local * rows + window],
            allowed,
        )
        block_rows.append(masked_max(score_max, operands))
    stacked = jnp.stack(block_rows, 0)[None]
    for level in range(2):
        partner = from_partner(stacked, "seq", level)
        upper = place // (1 << level) % 2 == 1
        stacked = jnp.where(
            upper, jnp.concatenate([partner, stacked], 0), jnp.concatenate([stacked, partner], 0)
        )
    own = lax.dynamic_index_in_dim(stacked, slot, 1, False)
    row_max = own.reshape(heads, rows).T
    local_heads = jnp.max(row_max, axis=0)
    head_max = lax.pmax(local_heads, "seq")
    return finish(threshold, head_max, row_max, w_q_nope, w_q_rope, w_kv_nope)


def finish(threshold, head_max, row_max, w_q_nope, w_q_rope, w_kv_nope):
    clip = threshold[0] / jnp.maximum(head_max, threshold[0])
    root = jnp.sqrt(clip)
    new_q_nope = (w_q_nope.astype(jnp.float32) * jnp.repeat(root, D_NOPE)[None, :]).astype(
        jnp.bfloat16
    )
    new_q_rope = (w_q_rope.astype(jnp.float32) * jnp.repeat(clip, D_ROPE)[None, :]).astype(
        jnp.bfloat16
    )
    new_kv_nope = (w_kv_nope.astype(jnp.float32) * jnp.repeat(root, D_NOPE)[None, :]).astype(
        jnp.bfloat16
    )
    return (new_q_nope, new_q_rope, new_kv_nope, head_max, row_max)


MESH = pl.DeviceIdType.MESH
LANES = 128


def other(index, stride):
    return index + stride - 2 * stride * (index // stride % 2)


def gather_kernel(
    n, m, q_lat, kv_lat, rope, segs, w_nope, w_rope, w_kv,
    q_all, kv_all, rope_all, segs_all, q_cols, kv_cols,
    own_q, own_kv, q_send, q_recv, kv_send, kv_recv, rope_send, rope_recv, seg_send, seg_recv,
    w_send, w_recv, local,
):
    s = lax.axis_index("seq")
    h = lax.axis_index("head")
    rows = q_lat.shape[0]
    part = rope.shape[0] // m
    nope_cols = w_nope.shape[1] // n
    rope_cols = w_rope.shape[1] // n
    kv_width = w_kv.shape[1] // n
    q_rows = w_nope.shape[0]
    kv_rows = w_kv.shape[0]

    strides = []
    stride = m // 2
    while stride >= 1:
        strides.append(stride)
        stride //= 2

    barrier = pltpu.get_barrier_semaphore()
    for k in range(1, n):
        pl.semaphore_signal(barrier, inc=1, device_id=(lax.rem(s + k, n), h), device_id_type=MESH)
    for stride in strides:
        pl.semaphore_signal(barrier, inc=1, device_id=(s, other(h, stride)), device_id_type=MESH)

    mine_nope = pl.ds(pl.multiple_of(s * nope_cols, LANES), nope_cols)
    mine_rope = pl.ds(pl.multiple_of(s * rope_cols, LANES), rope_cols)
    mine_kv = pl.ds(pl.multiple_of(s * kv_width, LANES), kv_width)
    loads = [
        pltpu.make_async_copy(w_nope.at[:, mine_nope], own_q.at[:, pl.ds(0, nope_cols)], local.at[0]),
        pltpu.make_async_copy(w_rope.at[:, mine_rope], own_q.at[:, pl.ds(nope_cols, rope_cols)], local.at[1]),
        pltpu.make_async_copy(w_kv.at[:, mine_kv], own_kv, local.at[2]),
    ]
    for copy in loads:
        copy.start()

    def window(whole, lat, ps, ph):
        width = lat.shape[1]
        return whole.at[pl.ds(pl.multiple_of(ps * rows, rows), rows), pl.ds(pl.multiple_of(ph * width, LANES), width)]

    def rope_at(ps, ph):
        return rope_all.at[ps, pl.ds(pl.multiple_of(ph * part, part), part), :]

    def places(ps, ph):
        return window(q_all, q_lat, ps, ph), window(kv_all, kv_lat, ps, ph), rope_at(ps, ph)

    mine = (q_lat, kv_lat, rope.at[pl.ds(pl.multiple_of(h * part, part), part), :])
    send_sems = (q_send, kv_send, rope_send)
    recv_sems = (q_recv, kv_recv, rope_recv)
    stores = [
        pltpu.make_async_copy(src, dst, local.at[3 + i])
        for i, (src, dst) in enumerate(zip(mine + (segs,), places(s, h) + (segs_all.at[s],)))
    ]
    for copy in stores:
        copy.start()
    pl.semaphore_wait(barrier, n - 1 + len(strides))

    sends = []
    slots = [0]

    def piece(ps, ph, target, own):
        slot = slots[0]
        slots[0] += 1
        copies = [
            pltpu.make_async_remote_copy(
                src_ref=src, dst_ref=dst, send_sem=sent.at[slot], recv_sem=got.at[ps * m + ph],
                device_id=target, device_id_type=MESH)
            for src, dst, sent, got in zip(
                mine if own else places(ps, ph), places(ps, ph), send_sems, recv_sems)
        ]
        for copy in copies:
            copy.start()

        def drain():
            for sent, src in zip(send_sems, mine):
                pltpu.make_async_copy(src, src, sent.at[slot]).wait()

        sends.append(drain)

    def arrive(ps, ph):
        for at, got in zip(places(ps, ph), recv_sems):
            pltpu.make_async_copy(at, at, got.at[ps * m + ph]).wait()

    others = []

    def weights(k):
        p = lax.rem(s + k, n)
        to = (p, h)
        q_at = pl.ds(pl.multiple_of(s * q_rows, q_rows), q_rows)
        kv_at = pl.ds(pl.multiple_of(s * kv_rows, kv_rows), kv_rows)
        pairs = (
            (w_nope.at[:, pl.ds(pl.multiple_of(p * nope_cols, LANES), nope_cols)], q_cols.at[q_at, pl.ds(0, nope_cols)]),
            (w_rope.at[:, pl.ds(pl.multiple_of(p * rope_cols, LANES), rope_cols)], q_cols.at[q_at, pl.ds(nope_cols, rope_cols)]),
            (w_kv.at[:, pl.ds(pl.multiple_of(p * kv_width, LANES), kv_width)], kv_cols.at[kv_at, :]),
        )
        for i, (src, dst) in enumerate(pairs):
            copy = pltpu.make_async_remote_copy(
                src_ref=src, dst_ref=dst, send_sem=w_send.at[i * n + k], recv_sem=w_recv.at[i * n + k],
                device_id=to, device_id_type=MESH)
            copy.start()
            others.append(copy)

    pair = other(s, 1)
    even = list(range(2, n, 2))

    for k in even:
        piece(s, h, (lax.rem(s + k, n), h), True)
    piece(s, h, (pair, h), True)
    for stride in strides:
        piece(s, h, (s, other(h, stride)), True)
    for k in range(1, n):
        copy = pltpu.make_async_remote_copy(
            src_ref=segs, dst_ref=segs_all.at[s], send_sem=seg_send.at[k], recv_sem=seg_recv.at[k],
            device_id=(lax.rem(s + k, n), h), device_id_type=MESH)
        copy.start()
        others.append(copy)
    for k in even:
        weights(k)
    for k in even:
        ps = lax.rem(s + n - k, n)
        arrive(ps, h)
        piece(ps, h, (pair, h), False)
        for stride in strides:
            piece(ps, h, (s, other(h, stride)), False)
    for k in range(1, n, 2):
        weights(k)
    for copy in loads:
        copy.wait()
    keep = [
        pltpu.make_async_copy(own_q, q_cols.at[pl.ds(pl.multiple_of(s * q_rows, q_rows), q_rows), :], local.at[7]),
        pltpu.make_async_copy(own_kv, kv_cols.at[pl.ds(pl.multiple_of(s * kv_rows, kv_rows), kv_rows), :], local.at[8]),
    ]
    for copy in keep:
        copy.start()
    for k in [0] + even:
        ps = lax.rem(pair + n - k, n)
        arrive(ps, h)
        for stride in strides:
            piece(ps, h, (s, other(h, stride)), False)
    held = [h]
    for i, stride in enumerate(strides):
        fresh = [other(ph, stride) for ph in held]
        for first in range(n):
            ps = lax.rem(s + first, n)
            for ph in fresh:
                arrive(ps, ph)
                for later in strides[i + 1:]:
                    piece(ps, ph, (s, other(h, later)), False)
        held = held + fresh
    for copy in others:
        copy.wait()
    for drain in sends:
        drain()
    for copy in stores + keep:
        copy.wait()


def gather_all(n, m, q_lat, kv_lat, rope, segs, w_nope, w_rope, w_kv):
    rows = q_lat.shape[0]
    q_width = (w_nope.shape[1] + w_rope.shape[1]) // n
    kv_width = w_kv.shape[1] // n
    moves = n // 2 - 1 + n * m
    any_ref = pl.BlockSpec(memory_space=pl.ANY)
    vmem = pl.BlockSpec(memory_space=pltpu.VMEM)
    dma = pltpu.SemaphoreType.DMA
    return pl.pallas_call(
        functools.partial(gather_kernel, n, m),
        out_shape=(
            jax.ShapeDtypeStruct((n * rows, m * q_lat.shape[1]), q_lat.dtype),
            jax.ShapeDtypeStruct((n * rows, m * kv_lat.shape[1]), kv_lat.dtype),
            jax.ShapeDtypeStruct((n,) + rope.shape, rope.dtype),
            jax.ShapeDtypeStruct((n,) + segs.shape, segs.dtype),
            jax.ShapeDtypeStruct((n * w_nope.shape[0], q_width), w_nope.dtype),
            jax.ShapeDtypeStruct((n * w_kv.shape[0], kv_width), w_kv.dtype),
        ),
        in_specs=[vmem, vmem, vmem, vmem, any_ref, any_ref, any_ref],
        out_specs=(any_ref,) * 6,
        scratch_shapes=[
            pltpu.VMEM((w_nope.shape[0], q_width), w_nope.dtype),
            pltpu.VMEM((w_kv.shape[0], kv_width), w_kv.dtype),
            dma((moves,)), dma((n * m,)), dma((moves,)), dma((n * m,)), dma((moves,)), dma((n * m,)),
            dma((n,)), dma((n,)),
            dma((3 * n,)), dma((3 * n,)), dma((9,)),
        ],
        compiler_params=pltpu.CompilerParams(collective_id=0, has_side_effects=True),
        name="gather_all",
    )(q_lat, kv_lat, rope, segs, w_nope, w_rope, w_kv)


def logit_kernel(own, q_lat, kv_lat, rope, segs, w_q, w_kv, out, keys, seg_cols):
    block = pl.program_id(0)
    rows = q_lat.shape[0]
    window = (REACH + 1) * rows
    q_scale = 1.0 / math.sqrt(QLORA)
    k_scale = 1.0 / math.sqrt(KVLORA)
    key = (jnp.dot(kv_lat[...], w_kv[...], preferred_element_type=jnp.float32) * k_scale).astype(jnp.bfloat16)
    query = (jnp.dot(q_lat[...], w_q[...], preferred_element_type=jnp.float32) * q_scale).astype(jnp.bfloat16)
    here = pl.ds(pl.multiple_of(block * rows, rows), rows)
    lane = lax.broadcasted_iota(jnp.int32, (rows, LANES), 1)
    turned = jnp.concatenate([rope[0].astype(jnp.float32)] * (LANES // D_ROPE), 0)
    twice = jnp.transpose(turned).astype(jnp.bfloat16)
    sides = [
        jnp.where(lane // D_ROPE == side, twice, jnp.zeros_like(twice)) for side in range(LANES // D_ROPE)
    ]
    for i in range(own):
        keys[i, here, :] = jnp.concatenate(
            [key[:, i * D_NOPE : (i + 1) * D_NOPE], sides[i % len(sides)]], 1
        )
    seg_row = segs[0]
    seg_cols[here, :] = jnp.transpose(jnp.broadcast_to(seg_row, (LANES, rows)))
    start = jnp.maximum(block - REACH, 0) * rows
    range_keys = pl.ds(pl.multiple_of(start, rows), window)
    key_segs = seg_cols[range_keys, :]
    key_segs = jnp.concatenate([key_segs] * (rows // LANES), 1)
    key_pos = start + lax.broadcasted_iota(jnp.int32, (window, rows), 0)
    query_pos = block * rows + lax.broadcasted_iota(jnp.int32, (window, rows), 1)
    allowed = (key_segs == seg_row) & (key_pos <= query_pos)
    base = own * D_NOPE
    found = []
    for i in range(own):
        pair = base + i // len(sides) * LANES
        q_head = jnp.concatenate(
            [query[:, i * D_NOPE : (i + 1) * D_NOPE], query[:, pair : pair + LANES]], 1
        )
        logits = lax.dot_general(
            keys[i, range_keys, :], q_head, (((1,), (1,)), ((), ())), preferred_element_type=jnp.float32
        )
        logits = jnp.where(allowed, logits, jnp.float32(-1e30))
        found.append(jnp.max(logits, axis=0, keepdims=True))
    out[0:own, here] = jnp.concatenate(found, 0) * (1.0 / math.sqrt(D_NOPE + D_ROPE))

    @pl.when(block == pl.num_programs(0) - 1)
    def _():
        top = jnp.max(out[0:own, :], axis=1, keepdims=True)
        out[own : 2 * own, :] = jnp.broadcast_to(top, (own, out.shape[1]))


def logit_maxima(n, own, q_lat, kv_lat, rope, segs, w_q, w_kv):
    rows = q_lat.shape[0] // n
    return pl.pallas_call(
        functools.partial(logit_kernel, own),
        grid=(n,),
        out_shape=jax.ShapeDtypeStruct((2 * own, q_lat.shape[0]), jnp.float32),
        in_specs=[
            pl.BlockSpec((rows, q_lat.shape[1]), lambda i: (i, 0)),
            pl.BlockSpec((rows, kv_lat.shape[1]), lambda i: (i, 0)),
            pl.BlockSpec((1,) + rope.shape[1:], lambda i: (i, 0, 0)),
            pl.BlockSpec((1,) + segs.shape[1:], lambda i: (i, 0, 0)),
            pl.BlockSpec(w_q.shape, lambda i: (0, 0)),
            pl.BlockSpec(w_kv.shape, lambda i: (0, 0)),
        ],
        out_specs=pl.BlockSpec((2 * own, q_lat.shape[0]), lambda i: (0, 0)),
        scratch_shapes=[
            pltpu.VMEM((own, q_lat.shape[0], D_NOPE + LANES), jnp.bfloat16),
            pltpu.VMEM((q_lat.shape[0], LANES), jnp.int32),
        ],
        compiler_params=pltpu.CompilerParams(dimension_semantics=("arbitrary",)),
        name="logit_maxima",
    )(q_lat, kv_lat, rope, segs, w_q, w_kv)


def exchange_kernel(n, maxima, out, send, recv):
    s = lax.axis_index("seq")
    h = lax.axis_index("head")
    rows = out.shape[2]
    barrier = pltpu.get_barrier_semaphore()
    for k in range(1, n):
        pl.semaphore_signal(barrier, inc=1, device_id=(lax.rem(s + k, n), h), device_id_type=MESH)
    pl.semaphore_wait(barrier, n - 1)
    copies = []
    for k in range(1, n):
        p = lax.rem(s + k, n)
        copy = pltpu.make_async_remote_copy(
            src_ref=maxima.at[:, pl.ds(pl.multiple_of(p * rows, rows), rows)], dst_ref=out.at[s],
            send_sem=send.at[k], recv_sem=recv.at[k], device_id=(p, h), device_id_type=MESH)
        copy.start()
        copies.append(copy)
    out[s] = maxima[:, pl.ds(pl.multiple_of(s * rows, rows), rows)]
    for copy in copies:
        copy.wait()


def exchange(n, maxima):
    vmem = pl.BlockSpec(memory_space=pltpu.VMEM)
    return pl.pallas_call(
        functools.partial(exchange_kernel, n),
        out_shape=jax.ShapeDtypeStruct((n, maxima.shape[0], maxima.shape[1] // n), jnp.float32),
        in_specs=[vmem],
        out_specs=vmem,
        scratch_shapes=[pltpu.SemaphoreType.DMA((n,)), pltpu.SemaphoreType.DMA((n,))],
        compiler_params=pltpu.CompilerParams(collective_id=1, has_side_effects=True),
        name="exchange",
    )(maxima)


def owned_body(n, m, q_latent, kv_latent, k_rope, segment_ids, w_q_nope, w_q_rope, w_kv_nope, threshold):
    rows = q_latent.shape[0]
    heads = w_q_nope.shape[1] // D_NOPE
    own = heads // n
    gathered = gather_all(
        n, m, q_latent, kv_latent, k_rope.T, segment_ids.reshape(1, rows), w_q_nope, w_q_rope, w_kv_nope
    )
    maxima = logit_maxima(n, own, *gathered)
    got = exchange(n, maxima)
    row_max = got[:, :own, :].reshape(heads, rows).T
    head_max = got[:, own:, 0].reshape(heads)
    return finish(threshold, head_max, row_max, w_q_nope, w_q_rope, w_kv_nope)


def body(n, m, *operands):
    heads = operands[4].shape[1] // D_NOPE
    rows = operands[0].shape[0]
    shares = heads % n == 0 and heads // n % (LANES // D_ROPE) == 0
    fits = n % 2 == 0 and n > REACH and m & (m - 1) == 0 and rows % LANES == 0 and operands[2].shape[1] % (16 * m) == 0
    if shares and fits and heads // n % 4 == 0:
        return owned_body(n, m, *operands)
    return grouped_body(*operands)


def solution(mesh):
    in_specs = (
        P("seq", "head"),
        P("seq", "head"),
        P("seq", None),
        P("seq"),
        P("seq", "head"),
        P("seq", "head"),
        P("seq", "head"),
        P(),
    )
    out_specs = (P("seq", "head"), P("seq", "head"), P("seq", "head"), P("head"), P("seq", "head"))
    return jax.shard_map(functools.partial(body, mesh.shape["seq"], mesh.shape["head"]), mesh=mesh, in_specs=in_specs, out_specs=out_specs, check_vma=False)
```

profile of v0, /device:TPU:0, one launch (start us, length us, event | category | flops | bytes accessed | tf_op | source)
XLA Modules:
  0.0 130.6 jit_solution(15503148180434036026)
XLA Ops:
  0.6 89.3 %gather_all.1 = (bf16[2048,1536]{1,0:T(8,128)(2,1)}, bf16[2048,512]{1,0:T(8,128)(2,1)}, bf16[8,64,256]{2,1,0:T(8,128)(2,1)}, s32[8,1,256]{2,1,0:T(1,128)}, bf16[...) custom-call(bf16[256,384]{1,0:T(8,128)(2,1)} %q_lat.1, bf16[256,128]{1,0:T(8,128)(2,1)} %kv_lat.1, ...), custom_call_target="tpu_custom_call" | custom-call | tf_op jit(solution)/shard_map/gather_all/pallas_call | solution.py:342
  89.9 0.0 copy-start
  89.9 20.8 %logit_maxima.1.maxima = f32[8,2048]{1,0:T(8,128)} custom-call(bf16[2048,1536]{1,0:T(8,128)(2,1)} %get-tuple-element.11.q_lat, bf16[2048,512]{1,0:T(8,128)(2,1)} %get-tuple-element.12.kv_lat, bf16[8,64,256]{2,1,0:T(8,128)(2,1)} %get-tuple-element.13.rope, s32[8,1,256]{2,1,0:T(1,128)} %get-tuple-element.14.segs, bf16[1536,768]{1,0:T(8,128)(2,1)} %get-tuple-element.15.w_q, ...), custom_call_target="tpu_custom_call" | custom-call | tf_op jit(solution)/shard_map/logit_maxima/pallas_call | solution.py:416
  110.7 14.0 %exchange.1 = f32[8,8,256]{2,1,0:T(8,128)} custom-call(f32[8,2048]{1,0:T(8,128)} %logit_maxima.1.maxima), custom_call_target="tpu_custom_call" | custom-call | tf_op jit(solution)/shard_map/exchange/pallas_call | solution.py:461
  124.8 0.8 slice_reduce_fusion
  125.6 0.1 reshape_squeeze.3
  125.7 0.0 copy-start.3
  126.4 0.1 broadcast_bitcast_fusion
  126.4 0.0 copy-done
  126.4 0.0 copy-start.2
  126.4 0.0 copy-start.1
  126.4 1.5 %multiply_convert_fusion = bf16[192,4096]{1,0:T(8,128)(2,1)} fusion(bf16[192,4096]{1,0:T(8,128)(2,1)S(1)} %copy-done, f32[4096]{0:T(1024)S(1)} %broadcast_bitcast_fusion), kind=kLoop, calls=%fused_computation | loop fusion | flops 2359296 | bytes 3162112 | tf_op jit(solution)/shard_map/convert_element_type | solution.py:154
  127.9 0.0 copy-done.3
  127.9 0.0 copy-done.2
  127.9 0.0 slice-start
  127.9 0.9 multiply_convert_fusion.2
  128.8 0.1 broadcast_in_dim.8
  128.9 0.1 mul.31
  128.9 0.0 copy-done.1
  128.9 1.0 multiply_convert_fusion.1
  130.0 0.0 slice-done
  130.0 0.6 reshape.19
  (1 shorter events, 0.0 us)
Async XLA Ops:
  89.9 36.5 %copy-start = (bf16[192,4096]{1,0:T(8,128)(2,1)S(1)}, bf16[192,4096]{1,0:T(8,128)(2,1)}, u32[]{:S(2)}) copy-start(bf16[192,4096]{1,0:T(8,128)(2,1)} %w_nope.1) | copy-start | bytes 4718596
  125.7 2.2 %copy-start.3 = (f32[32]{0:T(128)}, f32[32]{0:T(128)S(1)}, u32[]{:S(2)}) copy-start(f32[32]{0:T(128)S(1)} %reshape_squeeze.3) | copy-start | bytes 388
  126.4 1.5 %copy-start.2 = (bf16[64,4096]{1,0:T(8,128)(2,1)S(1)}, bf16[64,4096]{1,0:T(8,128)(2,1)}, u32[]{:S(2)}) copy-start(bf16[64,4096]{1,0:T(8,128)(2,1)} %w_kv.1) | copy-start | bytes 1572868
  126.4 2.5 %copy-start.1 = (bf16[192,2048]{1,0:T(8,128)(2,1)S(1)}, bf16[192,2048]{1,0:T(8,128)(2,1)}, u32[]{:S(2)}) copy-start(bf16[192,2048]{1,0:T(8,128)(2,1)} %w_rope.1) | copy-start | bytes 2359300
  127.9 2.1 %slice-start = ((f32[8,8,256]{2,1,0:T(8,128)}), f32[8,4,256]{2,1,0:T(4,128)S(1)}, s32[]{:S(2)}) async-start(f32[8,8,256]{2,1,0:T(8,128)} %exchange.1), calls=%async_computation | async-start | bytes 65536 | tf_op jit(solution)/shard_map/slice | solution.py:481
where the time goes:
time: 131 us
  Pallas kernels  124 us (95%)
  other arithmetic  3.39 us (3%)
  local copies, waits for them, and re-layouts  1.79 us (1%)
  between operations  1.33 us (1%)
    pallas_call x1, Pallas kernels, gather_all(): pl.pallas_call(functools.partial(gather_kernel, n, m), out_shape=(jax.Sha...  89.3 us
    pallas_call x1, Pallas kernels, logit_maxima(): pl.pallas_call(functools.partial(logit_kernel, own), grid=(n,), out_shape...  20.8 us
    pallas_call x1, Pallas kernels, exchange(): pl.pallas_call(functools.partial(exchange_kernel, n), out_shape=jax.Shape...  14 us

commit v1 on v0

v1 whole, which is shorter than its diff:
```python
import functools
import math

import jax
import jax.numpy as jnp
from jax import lax
from jax.experimental import pallas as pl
from jax.experimental.pallas import tpu as pltpu
from jax.sharding import PartitionSpec as P

D_NOPE = 128
D_ROPE = 64
QLORA = 1536
KVLORA = 512
REACH = 3


def as_sent(value):
    return jax.tree.map(lambda a: a.astype(jnp.bfloat16) if a.dtype == jnp.float32 else a, value)


def from_partner(value, axis, stride):
    mask = 2**stride
    pairs = [(source, source ^ mask) for source in range(lax.axis_size(axis))]
    return lax.ppermute(value, axis, pairs)


def shifted(block, axis, distance):
    devices = range(lax.axis_size(axis))
    route = [(i - distance, i) for i in devices if i - distance in devices]
    return lax.ppermute(block, axis, route)


def score_max(query_nope, query_rope, key_nope, key_rope, allowed):
    nope = jnp.einsum("qhd,khd->hqk", query_nope, key_nope, preferred_element_type=jnp.float32)
    rope = jnp.einsum("qhd,kd->hqk", query_rope, key_rope, preferred_element_type=jnp.float32)
    scores = (nope + rope) * (1.0 / math.sqrt(D_NOPE + D_ROPE))
    return jnp.max(jnp.where(allowed[None], scores, jnp.float32(-1e30)), axis=2)


def masked_max(compute, operands):
    return compute(*operands)


def spread_columns(weight, width, quarter, copies):
    pieces = weight.reshape(weight.shape[0], 4, quarter * width).transpose(1, 0, 2)
    return jnp.tile(pieces, (copies, 1, 1))


def grouped_body(q_latent, kv_latent, k_rope, segment_ids, w_q_nope, w_q_rope, w_kv_nope, threshold):
    q_whole, kv_whole = (
        lax.all_gather(q_latent, "head", axis=1, tiled=True),
        lax.all_gather(kv_latent, "head", axis=1, tiled=True),
    )
    rows = q_whole.shape[0]
    heads = w_q_nope.shape[1] // D_NOPE
    q_scale = 1.0 / math.sqrt(QLORA)
    k_scale = 1.0 / math.sqrt(KVLORA)
    place = lax.axis_index("seq")
    quarter = heads // 4
    copies = lax.axis_size("seq") // 4
    slot = place % 4
    sent = (
        spread_columns(w_q_nope, D_NOPE, quarter, copies),
        spread_columns(w_q_rope, D_ROPE, quarter, copies),
        spread_columns(w_kv_nope, D_NOPE, quarter, copies),
    )
    got_nope, got_rope, got_kv = (
        lax.all_to_all(sent[0], "seq", split_axis=0, concat_axis=1, tiled=True),
        lax.all_to_all(sent[1], "seq", split_axis=0, concat_axis=1, tiled=True),
        lax.all_to_all(sent[2], "seq", split_axis=0, concat_axis=1, tiled=True),
    )
    sub_nope = got_nope.reshape(QLORA, quarter * D_NOPE)
    sub_rope = got_rope.reshape(QLORA, quarter * D_ROPE)
    sub_kv = got_kv.reshape(KVLORA, quarter * D_NOPE)
    group = (q_whole, kv_whole, k_rope)
    for level in range(2):
        partner = jax.tree.map(
            lambda part, own: part.astype(own.dtype),
            from_partner(as_sent(group), "seq", level),
            group,
        )
        upper = place // (1 << level) % 2 == 1
        group = tuple(
            (
                jnp.where(
                    upper, jnp.concatenate([other, mine], 0), jnp.concatenate([mine, other], 0)
                )
                for mine, other in zip(group, partner)
            )
        )
    group_q, group_kv, group_rope = group
    early_kv, early_rope = shifted(
        (group_kv[(4 - REACH) * rows :], group_rope[(4 - REACH) * rows :]), "seq", 4
    )
    keys_kv = jnp.concatenate([early_kv, group_kv], 0)
    keys_rope = jnp.concatenate([early_rope, group_rope], 0)
    key_nope = (
        (jnp.dot(keys_kv, sub_kv, preferred_element_type=jnp.float32) * k_scale)
        .astype(jnp.bfloat16)
        .reshape(keys_kv.shape[0], quarter, D_NOPE)
    )
    query_nope = (
        (jnp.dot(group_q, sub_nope, preferred_element_type=jnp.float32) * q_scale)
        .astype(jnp.bfloat16)
        .reshape(4 * rows, quarter, D_NOPE)
    )
    query_rope = (
        (jnp.dot(group_q, sub_rope, preferred_element_type=jnp.float32) * q_scale)
        .astype(jnp.bfloat16)
        .reshape(4 * rows, quarter, D_ROPE)
    )
    all_segs = lax.all_gather(segment_ids, "seq", axis=0, tiled=True)
    padded_segs = jnp.concatenate([jnp.full((REACH * rows,), -1, jnp.int32), all_segs], 0)
    first = place // 4 * 4
    window = (REACH + 1) * rows
    block_rows = []
    for local in range(4):
        block = first + local
        query_seg = lax.dynamic_slice_in_dim(all_segs, block * rows, rows, 0)
        key_seg = lax.dynamic_slice_in_dim(padded_segs, block * rows, window, 0)
        query_pos = block * rows + jnp.arange(rows, dtype=jnp.int32)
        key_pos = (block - REACH) * rows + jnp.arange(window, dtype=jnp.int32)
        allowed = (
            (query_seg[:, None] == key_seg[None, :])
            & (key_pos[None, :] <= query_pos[:, None])
            & (key_pos[None, :] >= 0)
        )
        operands = (
            query_nope[local * rows : (local + 1) * rows],
            query_rope[local * rows : (local + 1) * rows],
            key_nope[local * rows : local * rows + window],
            keys_rope[local * rows : local * rows + window],
            allowed,
        )
        block_rows.append(masked_max(score_max, operands))
    stacked = jnp.stack(block_rows, 0)[None]
    for level in range(2):
        partner = from_partner(stacked, "seq", level)
        upper = place // (1 << level) % 2 == 1
        stacked = jnp.where(
            upper, jnp.concatenate([partner, stacked], 0), jnp.concatenate([stacked, partner], 0)
        )
    own = lax.dynamic_index_in_dim(stacked, slot, 1, False)
    row_max = own.reshape(heads, rows).T
    local_heads = jnp.max(row_max, axis=0)
    head_max = lax.pmax(local_heads, "seq")
    return finish(threshold, head_max, row_max, w_q_nope, w_q_rope, w_kv_nope)


def finish(threshold, head_max, row_max, w_q_nope, w_q_rope, w_kv_nope):
    clip = threshold[0] / jnp.maximum(head_max, threshold[0])
    root = jnp.sqrt(clip)
    new_q_nope = (w_q_nope.astype(jnp.float32) * jnp.repeat(root, D_NOPE)[None, :]).astype(
        jnp.bfloat16
    )
    new_q_rope = (w_q_rope.astype(jnp.float32) * jnp.repeat(clip, D_ROPE)[None, :]).astype(
        jnp.bfloat16
    )
    new_kv_nope = (w_kv_nope.astype(jnp.float32) * jnp.repeat(root, D_NOPE)[None, :]).astype(
        jnp.bfloat16
    )
    return (new_q_nope, new_q_rope, new_kv_nope, head_max, row_max)


MESH = pl.DeviceIdType.MESH
LANES = 128


def other(index, stride):
    return index + stride - 2 * stride * (index // stride % 2)


def flip(index, bits):
    stride = 1
    while stride <= bits:
        if bits & stride:
            index = other(index, stride)
        stride *= 2
    return index


def halvings(size):
    return [size >> (i + 1) for i in range(size.bit_length() - 1)]


def layer_kernel(
    n, m, own, q_lat, kv_lat, rope, segs, w_nope, w_rope, w_kv, got,
    q_all, kv_all, rope_all, segs_all, w_even, w_odd, w_key, keys, caps, seg_cols, pair_rope, near_sum, maxima,
    q_send, q_recv, kv_send, kv_recv, rope_send, rope_recv, seg_send, seg_recv, w_send, w_recv, max_send, max_recv, local,
):
    s = lax.axis_index("seq")
    h = lax.axis_index("head")
    rows = q_lat.shape[0]
    part = rope.shape[0] // m
    pairs = own // 2
    q_rows = w_nope.shape[0]
    kv_rows = w_kv.shape[0]
    half = n // 2
    routes = [("seq", stride) for stride in halvings(n)] + [("head", stride) for stride in halvings(m)]
    last = len([1 for axis, _ in routes if axis == "seq"])

    barrier = pltpu.get_barrier_semaphore()
    for k in range(1, n):
        pl.semaphore_signal(barrier, inc=1, device_id=(flip(s, k), h), device_id_type=MESH)
    for stride in halvings(m):
        pl.semaphore_signal(barrier, inc=1, device_id=(s, other(h, stride)), device_id_type=MESH)

    def window(whole, width, ps, ph):
        return whole.at[pl.ds(pl.multiple_of(ps * rows, rows), rows), pl.ds(pl.multiple_of(ph * width, LANES), width)]

    def places(k, g):
        ps, ph = flip(s, k), flip(h, g)
        return (
            window(q_all, q_lat.shape[1], ps, ph),
            window(kv_all, kv_lat.shape[1], ps, ph),
            rope_all.at[ps, pl.ds(pl.multiple_of(ph * part, part), part), :],
        )

    def parts_of(p):
        found = []
        for j in range(pairs):
            even = pl.ds(pl.multiple_of((p * own + 2 * j) * LANES, LANES), LANES)
            odd = pl.ds(pl.multiple_of((p * own + 2 * j + 1) * LANES, LANES), LANES)
            both = pl.ds(pl.multiple_of((p * pairs + j) * LANES, LANES), LANES)
            found.append((w_nope.at[:, even], w_even, j, slice(0, LANES)))
            found.append((w_rope.at[:, both], w_even, j, slice(LANES, 2 * LANES)))
            found.append((w_nope.at[:, odd], w_odd, j, slice(0, LANES)))
        found.append((w_kv.at[:, pl.ds(pl.multiple_of(p * own * LANES, LANES), own * LANES)], w_key, None, None))
        return found

    def landing(target, j, columns, source):
        if j is None:
            return target.at[pl.ds(pl.multiple_of(source * kv_rows, kv_rows), kv_rows), :]
        return target.at[j, pl.ds(pl.multiple_of(source * q_rows, q_rows), q_rows), columns]

    own_pieces = (q_lat, kv_lat, rope.at[pl.ds(pl.multiple_of(h * part, part), part), :], segs)
    loads = [
        pltpu.make_async_copy(src, dst, local.at[i])
        for i, (src, dst) in enumerate(zip(own_pieces, places(0, 0) + (segs_all.at[s],)))
    ]
    for copy in loads:
        copy.start()
    keeps = [
        pltpu.make_async_copy(src, landing(target, j, columns, s), local.at[4 + i])
        for i, (src, target, j, columns) in enumerate(parts_of(s))
    ]
    for copy in keeps:
        copy.start()
    pl.semaphore_wait(barrier, n - 1 + len(halvings(m)))
    for copy in loads:
        copy.wait()

    drains = []
    slots = [0]

    def push(k, g, route):
        axis, stride = route
        target = (other(s, stride), h) if axis == "seq" else (s, other(h, stride))
        at = (k ^ stride) * m + g if axis == "seq" else k * m + (g ^ stride)
        slot = slots[0]
        slots[0] += 1
        for ref, sent, taken in zip(places(k, g), (q_send, kv_send, rope_send), (q_recv, kv_recv, rope_recv)):
            copy = pltpu.make_async_remote_copy(
                src_ref=ref, dst_ref=ref, send_sem=sent.at[slot], recv_sem=taken.at[at],
                device_id=target, device_id_type=MESH)
            copy.start()
            drains.append((ref, sent.at[slot]))

    def relay(k, g):
        for ref, taken in zip(places(k, g), (q_recv, kv_recv, rope_recv)):
            pltpu.make_async_copy(ref, ref, taken.at[k * m + g]).wait()
        reached = max(i for i, (axis, stride) in enumerate(routes) if (k if axis == "seq" else g) & stride)
        for route in routes[reached + 1:]:
            push(k, g, route)

    def weights(wanted, k):
        p = flip(s, k)
        for i, (src, target, j, columns) in enumerate(parts_of(p)):
            if i in wanted:
                copy = pltpu.make_async_remote_copy(
                    src_ref=src, dst_ref=landing(target, j, columns, s),
                    send_sem=w_send.at[i * n + k], recv_sem=w_recv.at[i * n + k],
                    device_id=(p, h), device_id_type=MESH)
                copy.start()
                drains.append((src, w_send.at[i * n + k]))

    def take(wanted, ks):
        for k in ks:
            for i, (_, target, j, columns) in enumerate(parts_of(s)):
                if i in wanted:
                    ref = landing(target, j, columns, flip(s, k))
                    pltpu.make_async_copy(ref, ref, w_recv.at[i * n + k]).wait()

    far = [k ^ half for k in range(half)]
    near = list(range(half - 1, 0, -1))
    kv_part = 3 * pairs
    first = [0, 1]
    later = [[kv_part]] + [[2]] + [group for j in range(1, pairs) for group in ([3 * j, 3 * j + 1], [3 * j + 2])]

    for route in routes:
        push(0, 0, route)
    for k in range(1, n):
        copy = pltpu.make_async_remote_copy(
            src_ref=segs_all.at[s], dst_ref=segs_all.at[s], send_sem=seg_send.at[k], recv_sem=seg_recv.at[k],
            device_id=(flip(s, k), h), device_id_type=MESH)
        copy.start()
        drains.append((segs_all.at[s], seg_send.at[k]))
    for k in far:
        weights(first, k)
    order = sorted(range(1, n), key=lambda k: (bin(k).count("1"), k & 1 == 1 and bin(k).count("1") > 1, k))
    on_links = max(i for i, k in enumerate(order) if k & 1 == 0)
    for k in order[: on_links + 1]:
        relay(k, 0)
    for k in near:
        weights(first, k)
    for wanted in later:
        for k in far + near:
            weights(wanted, k)

    for k in range(1, n):
        ref = segs_all.at[flip(s, k)]
        pltpu.make_async_copy(ref, ref, seg_recv.at[k]).wait()

    def fill_segs(block, carry):
        here = pl.ds(pl.multiple_of(block * rows, rows), rows)
        seg_cols[here, :] = jnp.transpose(jnp.broadcast_to(segs_all[block], (LANES, rows)))
        return carry

    lax.fori_loop(0, n, fill_segs, 0)
    reach = (REACH + 1) * rows

    def range_of(block):
        start = jnp.maximum(block - REACH, 0) * rows
        return start, pl.ds(pl.multiple_of(start, rows), reach)

    def fill_caps(block, carry):
        start, span = range_of(block)
        key_segs = jnp.concatenate([seg_cols[span, :]] * (rows // LANES), 1)
        key_pos = start + lax.broadcasted_iota(jnp.int32, (reach, rows), 0)
        query_pos = block * rows + lax.broadcasted_iota(jnp.int32, (reach, rows), 1)
        allowed = (key_segs == segs_all[block]) & (key_pos <= query_pos)
        caps[block] = jnp.where(allowed, jnp.float32(3.4e38), jnp.float32(-1e30))
        return carry

    lax.fori_loop(0, n, fill_caps, 0)

    for k in order[on_links + 1:]:
        relay(k, 0)
    for g in range(1, m):
        for k in [0] + order:
            relay(k, g)

    for copy in keeps:
        copy.wait()
    take([kv_part], far + near)
    q_scale = 1.0 / math.sqrt(QLORA)
    k_scale = 1.0 / math.sqrt(KVLORA)
    lane = lax.broadcasted_iota(jnp.int32, (rows, LANES), 1)
    sides = LANES // D_ROPE

    def fill_keys(block, carry):
        here = pl.ds(pl.multiple_of(block * rows, rows), rows)
        key = (jnp.dot(kv_all[here, :], w_key[...], preferred_element_type=jnp.float32) * k_scale).astype(jnp.bfloat16)
        turned = jnp.concatenate([rope_all[block].astype(jnp.float32)] * sides, 0)
        twice = jnp.transpose(turned).astype(jnp.bfloat16)
        for i in range(own):
            side = jnp.where(lane // D_ROPE == i % sides, twice, jnp.zeros_like(twice))
            keys[i, here, :] = jnp.concatenate([key[:, i * D_NOPE : (i + 1) * D_NOPE], side], 1)
        return carry

    lax.fori_loop(0, n, fill_keys, 0)

    def top_logits(i, block, q_head):
        here = pl.ds(pl.multiple_of(block * rows, rows), rows)
        _, span = range_of(block)
        logits = lax.dot_general(
            keys[i, span, :], q_head, (((1,), (1,)), ((), ())), preferred_element_type=jnp.float32
        )
        top = jnp.max(jnp.minimum(logits, caps[block]), axis=0, keepdims=True)
        maxima[i : i + 1, here] = top * (1.0 / math.sqrt(D_NOPE + D_ROPE))

    depth = half * q_rows
    close = pl.multiple_of(s // half * depth, depth)
    distant = pl.multiple_of((1 - s // half) * depth, depth)

    for j in range(pairs):
        take([3 * j, 3 * j + 1], far + near)

        def even_head(block, carry):
            here = pl.ds(pl.multiple_of(block * rows, rows), rows)
            query = jnp.dot(q_all[here, :], w_even[j], preferred_element_type=jnp.float32)
            query = (query * q_scale).astype(jnp.bfloat16)
            pair_rope[here, :] = query[:, LANES:]
            top_logits(2 * j, block, query)
            return carry

        lax.fori_loop(0, n, even_head, 0)
        take([3 * j + 2], near)

        def odd_near(block, carry):
            here = pl.ds(pl.multiple_of(block * rows, rows), rows)
            near_sum[here, :] = jnp.dot(
                q_all[here, pl.ds(close, depth)], w_odd[j, pl.ds(close, depth), :], preferred_element_type=jnp.float32
            )
            return carry

        lax.fori_loop(0, n, odd_near, 0)
        take([3 * j + 2], far)

        def odd_head(block, carry):
            here = pl.ds(pl.multiple_of(block * rows, rows), rows)
            query = near_sum[here, :] + jnp.dot(
                q_all[here, pl.ds(distant, depth)], w_odd[j, pl.ds(distant, depth), :], preferred_element_type=jnp.float32
            )
            query = (query * q_scale).astype(jnp.bfloat16)
            top_logits(2 * j + 1, block, jnp.concatenate([query, pair_rope[here, :]], 1))
            return carry

        lax.fori_loop(0, n, odd_head, 0)

    best = jnp.max(maxima[0:own, :], axis=1, keepdims=True)
    maxima[own : 2 * own, :] = jnp.broadcast_to(best, (own, maxima.shape[1]))
    shares = []
    for k in range(1, n):
        p = flip(s, k)
        copy = pltpu.make_async_remote_copy(
            src_ref=maxima.at[:, pl.ds(pl.multiple_of(p * rows, rows), rows)], dst_ref=got.at[s],
            send_sem=max_send.at[k], recv_sem=max_recv.at[k], device_id=(p, h), device_id_type=MESH)
        copy.start()
        shares.append(copy)
    got[s] = maxima[:, pl.ds(pl.multiple_of(s * rows, rows), rows)]
    for ref, sent in drains:
        pltpu.make_async_copy(ref, ref, sent).wait()
    for k, copy in zip(range(1, n), shares):
        copy.wait_send()
        at = got.at[flip(s, k)]
        pltpu.make_async_copy(at, at, max_recv.at[k]).wait()


def layer(n, m, own, q_lat, kv_lat, rope, segs, w_nope, w_rope, w_kv):
    rows = q_lat.shape[0]
    tokens = n * rows
    pairs = own // 2
    moves = n * m - 1
    parts = 3 * pairs + 1
    any_ref = pl.BlockSpec(memory_space=pl.ANY)
    dma = pltpu.SemaphoreType.DMA
    kind = q_lat.dtype
    return pl.pallas_call(
        functools.partial(layer_kernel, n, m, own),
        out_shape=jax.ShapeDtypeStruct((n, 2 * own, rows), jnp.float32),
        in_specs=[any_ref] * 7,
        out_specs=pl.BlockSpec(memory_space=pltpu.VMEM),
        scratch_shapes=[
            pltpu.VMEM((tokens, m * q_lat.shape[1]), kind),
            pltpu.VMEM((tokens, m * kv_lat.shape[1]), kind),
            pltpu.VMEM((n,) + rope.shape, kind),
            pltpu.VMEM((n,) + segs.shape, jnp.int32),
            pltpu.VMEM((pairs, n * w_nope.shape[0], 2 * LANES), kind),
            pltpu.VMEM((pairs, n * w_nope.shape[0], LANES), kind),
            pltpu.VMEM((n * w_kv.shape[0], own * LANES), kind),
            pltpu.VMEM((own, tokens, D_NOPE + LANES), kind),
            pltpu.VMEM((n, (REACH + 1) * rows, rows), jnp.float32),
            pltpu.VMEM((tokens, LANES), jnp.int32),
            pltpu.VMEM((tokens, LANES), kind),
            pltpu.VMEM((tokens, LANES), jnp.float32),
            pltpu.VMEM((2 * own, tokens), jnp.float32),
            dma((moves,)), dma((n * m,)), dma((moves,)), dma((n * m,)), dma((moves,)), dma((n * m,)),
            dma((n,)), dma((n,)),
            dma((parts * n,)), dma((parts * n,)), dma((n,)), dma((n,)), dma((4 + parts,)),
        ],
        compiler_params=pltpu.CompilerParams(
            collective_id=0, has_side_effects=True, vmem_limit_bytes=44 * 1024 * 1024
        ),
        name="layer",
    )(q_lat, kv_lat, rope, segs, w_nope, w_rope, w_kv)


def clip_kernel(n, own, got, threshold, w_nope, w_rope, w_kv, new_nope, new_rope, new_kv, head_max, row_max):
    limit = threshold[0]
    lane = lax.broadcasted_iota(jnp.int32, (1, LANES), 1)
    tops = jnp.zeros((1, head_max.shape[1]), jnp.float32)
    place = lax.broadcasted_iota(jnp.int32, tops.shape, 1)

    def scaled(source, target, columns, factor):
        target[:, columns] = (source[:, columns].astype(jnp.float32) * factor).astype(target.dtype)

    for s in range(n):
        top = got[s, own : 2 * own, 0:LANES]
        clip = limit / jnp.maximum(top, limit)
        root = jnp.sqrt(clip)
        for i in range(own):
            head = s * own + i
            columns = slice(head * LANES, (head + 1) * LANES)
            scaled(w_nope, new_nope, columns, root[i : i + 1])
            scaled(w_kv, new_kv, columns, root[i : i + 1])
            tops = jnp.where(place == head, top[i : i + 1, 0 : tops.shape[1]], tops)
        for j in range(own // 2):
            pair = s * own // 2 + j
            columns = slice(pair * LANES, (pair + 1) * LANES)
            factor = jnp.where(lane < D_ROPE, clip[2 * j : 2 * j + 1], clip[2 * j + 1 : 2 * j + 2])
            scaled(w_rope, new_rope, columns, factor)
        row_max[s * own : (s + 1) * own, :] = got[s, 0:own, :]
    head_max[...] = tops


def clip_weights(n, own, got, threshold, w_nope, w_rope, w_kv):
    steps = 4 if w_nope.shape[0] % 64 == 0 and w_kv.shape[0] % 64 == 0 else 1
    weights = (w_nope, w_rope, w_kv)
    blocks = [pl.BlockSpec((w.shape[0] // steps, w.shape[1]), lambda i: (i, 0)) for w in weights]
    heads = n * own
    return pl.pallas_call(
        functools.partial(clip_kernel, n, own),
        grid=(steps,),
        out_shape=tuple(jax.ShapeDtypeStruct(w.shape, w.dtype) for w in weights)
        + (jax.ShapeDtypeStruct((1, heads), jnp.float32), jax.ShapeDtypeStruct((heads, got.shape[2]), jnp.float32)),
        in_specs=[pl.BlockSpec(got.shape, lambda i: (0, 0, 0)), pl.BlockSpec(memory_space=pltpu.SMEM)] + blocks,
        out_specs=tuple(blocks)
        + (pl.BlockSpec((1, heads), lambda i: (0, 0)), pl.BlockSpec((heads, got.shape[2]), lambda i: (0, 0))),
        compiler_params=pltpu.CompilerParams(dimension_semantics=("arbitrary",)),
        name="clip_weights",
    )(got, threshold, w_nope, w_rope, w_kv)


def owned_body(n, m, q_latent, kv_latent, k_rope, segment_ids, w_q_nope, w_q_rope, w_kv_nope, threshold):
    rows = q_latent.shape[0]
    heads = w_q_nope.shape[1] // D_NOPE
    own = heads // n
    got = layer(n, m, own, q_latent, kv_latent, k_rope.T, segment_ids.reshape(1, rows), w_q_nope, w_q_rope, w_kv_nope)
    new_nope, new_rope, new_kv, head_max, row_max = clip_weights(n, own, got, threshold, w_q_nope, w_q_rope, w_kv_nope)
    return (new_nope, new_rope, new_kv, head_max.reshape(heads), row_max.T)


def body(n, m, *operands):
    heads = operands[4].shape[1] // D_NOPE
    rows = operands[0].shape[0]
    shares = heads % n == 0 and heads // n % 4 == 0 and heads <= LANES
    powers = n & (n - 1) == 0 and m & (m - 1) == 0 and n > REACH
    small = n * rows * operands[0].shape[1] * m <= 2048 * 1536
    if shares and powers and small and rows % LANES == 0 and operands[2].shape[1] % (16 * m) == 0:
        return owned_body(n, m, *operands)
    return grouped_body(*operands)


def solution(mesh):
    in_specs = (
        P("seq", "head"),
        P("seq", "head"),
        P("seq", None),
        P("seq"),
        P("seq", "head"),
        P("seq", "head"),
        P("seq", "head"),
        P(),
    )
    out_specs = (P("seq", "head"), P("seq", "head"), P("seq", "head"), P("head"), P("seq", "head"))
    return jax.shard_map(functools.partial(body, mesh.shape["seq"], mesh.shape["head"]), mesh=mesh, in_specs=in_specs, out_specs=out_specs, check_vma=False)
```

time: 131 us -> 112 us (0.85)
  Pallas kernels: 124 us -> 103 us
  local copies, waits for them, and re-layouts: 1.79 us -> 7.4 us
  other arithmetic: 3.39 us -> 0 us
    pallas_call x3 -> x2, Pallas kernels: 124 us -> 103 us  [the longest x1 98.6 us: layer(): pl.pallas_call(functools.partial(layer_kernel, n, m, own), out_shape=jax....]
    unnamed x8 -> x16, local copies, waits for them, and re-layouts: 0.02 us -> 7.4 us
    convert_element_type x3 -> x0, other arithmetic: 3.38 us -> none  [the longest x1 1.46 us: finish(): (w_q_nope.astype(jnp.float32) * jnp.repeat(root, D_NOPE)[None, :]).astype...]
where the time goes in v1:
time: 112 us
  Pallas kernels  103 us (92%)
  local copies, waits for them, and re-layouts  7.4 us (7%)
  between operations  1.31 us (1%)
    pallas_call x1, Pallas kernels, layer(): pl.pallas_call(functools.partial(layer_kernel, n, m, own), out_shape=jax....  98.6 us
    unnamed x16, local copies, waits for them, and re-layouts  7.4 us
    pallas_call x1, Pallas kernels, clip_weights(): pl.pallas_call(functools.partial(clip_kernel, n, own), grid=(steps,), out...  4.24 us

profile of v1, /device:TPU:0, one launch (start us, length us, event | category | flops | bytes accessed | tf_op | source)
XLA Modules:
  0.0 111.6 jit_solution(4864687160742991907)
XLA Ops:
  1.3 0.0 copy-start
  1.3 1.4 %copy-done = bf16[192,4096]{1,0:T(8,128)(2,1)S(1)} copy-done((bf16[192,4096]{1,0:T(8,128)(2,1)S(1)}, bf16[192,4096]{1,0:T(8,128)(2,1)}, u32[]{:S(2)}) %copy-start) | copy-done | bytes 1572888
  2.7 0.0 copy-start.1
  2.7 1.1 %copy-done.1 = bf16[192,2048]{1,0:T(8,128)(2,1)S(1)} copy-done((bf16[192,2048]{1,0:T(8,128)(2,1)S(1)}, bf16[192,2048]{1,0:T(8,128)(2,1)}, u32[]{:S(2)}) %copy-start.1) | copy-done | bytes 786456
  3.8 0.0 copy-start.2
  3.8 1.0 copy-done.2
  4.9 0.0 copy-start.4
  4.9 0.9 copy-done.4
  5.8 0.0 copy-start.5
  5.8 0.8 copy-done.5
  6.6 0.0 copy-start.6
  6.6 0.8 copy-done.6
  7.4 0.0 copy-start.7
  7.4 0.7 copy-done.7
  8.1 98.6 %layer.1.got = f32[8,8,256]{2,1,0:T(8,128)S(1)} custom-call(bf16[256,384]{1,0:T(8,128)(2,1)S(1)} %copy-done.4, bf16[256,128]{1,0:T(8,128)(2,1)S(1)} %copy-done.5, bf16[64,256]{1,0:T(8,128)(2,1)S(1)} %bitcast.4, s32[1,256]{1,0:T(1,128)S(1)} %bitcast.5, bf16[192,4096]{1,0:T(8,128)(2,1)S(1)} %copy-done, bf16[192,2048]{1,0:T(8,128)(2,1)S(1)} %copy-done.1, ...), custom_call_target="tpu_custom_call" | custom-call | tf_op jit(solution)/shard_map/layer/pallas_call | solution.py:450
  106.7 0.0 copy-start.3
  106.7 0.6 copy-done.3
  107.3 4.2 %clip_weights.1 = (bf16[192,4096]{1,0:T(8,128)(2,1)}, bf16[192,2048]{1,0:T(8,128)(2,1)}, bf16[64,4096]{1,0:T(8,128)(2,1)}, f32[1,32]{1,0:T(1,128)}, f32[32,256]{1,0:T(8,128)}) custom-call(f32[8,8,256]{2,1,0:T(8,128)} %copy-done.3, f32[1]{0:T(128)S(6)} %copy.13.threshold, bf16[192,4096]{1,0:T(8,128)(2,1)} %w_nope.3, bf16[192,2048]{1,0:T(8,128)(2,1)} %w_rope.3, ...), custom_call_target="tpu_custom_call" | custom-call | tf_op jit(solution)/shard_map/clip_weights/pallas_call | solution.py:513
Async XLA Ops:
  1.3 1.4 %copy-start = (bf16[192,4096]{1,0:T(8,128)(2,1)S(1)}, bf16[192,4096]{1,0:T(8,128)(2,1)}, u32[]{:S(2)}) copy-start(bf16[192,4096]{1,0:T(8,128)(2,1)} %w_nope.3) | copy-start | bytes 4718596
  2.7 1.1 %copy-start.1 = (bf16[192,2048]{1,0:T(8,128)(2,1)S(1)}, bf16[192,2048]{1,0:T(8,128)(2,1)}, u32[]{:S(2)}) copy-start(bf16[192,2048]{1,0:T(8,128)(2,1)} %w_rope.3) | copy-start | bytes 2359300
  3.8 1.0 copy-start.2
  4.9 0.9 copy-start.4
  5.8 0.8 copy-start.5
  6.6 0.8 copy-start.6
  7.4 0.7 copy-start.7
  106.7 0.6 copy-start.3

commit v2 on v1

--- a/solution.py
+++ b/solution.py
@@ -185,8 +185,8 @@
 
 
 def layer_kernel(
-    n, m, own, q_lat, kv_lat, rope, segs, w_nope, w_rope, w_kv, got,
-    q_all, kv_all, rope_all, segs_all, w_even, w_odd, w_key, keys, caps, seg_cols, pair_rope, near_sum, maxima,
+    n, m, own, q_lat, kv_lat, rope, segs, w_nope, w_rope, w_kv, got, held_nope, held_rope, held_kv,
+    q_all, kv_all, rope_all, segs_all, w_even, w_odd, w_key, keys, caps, seg_cols, queries, near_sum, maxima,
     q_send, q_recv, kv_send, kv_recv, rope_send, rope_recv, seg_send, seg_recv, w_send, w_recv, max_send, max_recv, local,
 ):
     s = lax.axis_index("seq")
@@ -244,6 +244,9 @@
     keeps = [
         pltpu.make_async_copy(src, landing(target, j, columns, s), local.at[4 + i])
         for i, (src, target, j, columns) in enumerate(parts_of(s))
+    ] + [
+        pltpu.make_async_copy(src, dst, local.at[4 + len(parts_of(s)) + i])
+        for i, (src, dst) in enumerate(zip((w_nope, w_rope, w_kv), (held_nope, held_rope, held_kv)))
     ]
     for copy in keeps:
         copy.start()
@@ -285,12 +288,12 @@
                 copy.start()
                 drains.append((src, w_send.at[i * n + k]))
 
-    def take(wanted, ks):
+    def take(j, wanted, ks):
         for k in ks:
-            for i, (_, target, j, columns) in enumerate(parts_of(s)):
-                if i in wanted:
-                    ref = landing(target, j, columns, flip(s, k))
-                    pltpu.make_async_copy(ref, ref, w_recv.at[i * n + k]).wait()
+            for i in wanted:
+                target, columns = ((w_even, slice(0, LANES)), (w_even, slice(LANES, 2 * LANES)), (w_odd, slice(0, LANES)))[i]
+                ref = landing(target, j, columns, flip(s, k))
+                pltpu.make_async_copy(ref, ref, w_recv.at[(3 * j + i) * n + k]).wait()
 
     far = [k ^ half for k in range(half)]
     near = list(range(half - 1, 0, -1))
@@ -353,7 +356,9 @@
 
     for copy in keeps:
         copy.wait()
-    take([kv_part], far + near)
+    for k in far + near:
+        ref = landing(w_key, None, None, flip(s, k))
+        pltpu.make_async_copy(ref, ref, w_recv.at[kv_part * n + k]).wait()
     q_scale = 1.0 / math.sqrt(QLORA)
     k_scale = 1.0 / math.sqrt(KVLORA)
     lane = lax.broadcasted_iota(jnp.int32, (rows, LANES), 1)
@@ -372,52 +377,49 @@
     lax.fori_loop(0, n, fill_keys, 0)
 
     def top_logits(i, block, q_head):
-        here = pl.ds(pl.multiple_of(block * rows, rows), rows)
-        _, span = range_of(block)
-        logits = lax.dot_general(
-            keys[i, span, :], q_head, (((1,), (1,)), ((), ())), preferred_element_type=jnp.float32
-        )
-        top = jnp.max(jnp.minimum(logits, caps[block]), axis=0, keepdims=True)
-        maxima[i : i + 1, here] = top * (1.0 / math.sqrt(D_NOPE + D_ROPE))
+        first = max(block - REACH, 0)
+        best = None
+        for other_block in range(first, block + 1):
+            logits = lax.dot_general(
+                keys[i, other_block * rows : (other_block + 1) * rows, :], q_head,
+                (((1,), (1,)), ((), ())), preferred_element_type=jnp.float32,
+            )
+            cap = caps[block, (other_block - first) * rows : (other_block - first + 1) * rows, :]
+            top = jnp.max(jnp.minimum(logits, cap).reshape(rows // 8, 8, rows), axis=0)
+            best = top if best is None else jnp.maximum(best, top)
+        top = jnp.max(best, axis=0, keepdims=True) * (1.0 / math.sqrt(D_NOPE + D_ROPE))
+        maxima[pl.ds(i, 1), block * rows : (block + 1) * rows] = top
 
     depth = half * q_rows
     close = pl.multiple_of(s // half * depth, depth)
     distant = pl.multiple_of((1 - s // half) * depth, depth)
 
-    for j in range(pairs):
-        take([3 * j, 3 * j + 1], far + near)
-
-        def even_head(block, carry):
-            here = pl.ds(pl.multiple_of(block * rows, rows), rows)
+    def head_pair(j, carry):
+        take(j, (0, 1), far + near)
+        for block in range(n):
+            here = slice(block * rows, (block + 1) * rows)
             query = jnp.dot(q_all[here, :], w_even[j], preferred_element_type=jnp.float32)
-            query = (query * q_scale).astype(jnp.bfloat16)
-            pair_rope[here, :] = query[:, LANES:]
-            top_logits(2 * j, block, query)
-            return carry
-
-        lax.fori_loop(0, n, even_head, 0)
-        take([3 * j + 2], near)
-
-        def odd_near(block, carry):
-            here = pl.ds(pl.multiple_of(block * rows, rows), rows)
+            queries[here, :] = (query * q_scale).astype(jnp.bfloat16)
+        for block in range(n):
+            top_logits(2 * j, block, queries[block * rows : (block + 1) * rows, :])
+        take(j, (2,), near)
+        for block in range(n):
+            here = slice(block * rows, (block + 1) * rows)
             near_sum[here, :] = jnp.dot(
                 q_all[here, pl.ds(close, depth)], w_odd[j, pl.ds(close, depth), :], preferred_element_type=jnp.float32
             )
-            return carry
-
-        lax.fori_loop(0, n, odd_near, 0)
-        take([3 * j + 2], far)
-
-        def odd_head(block, carry):
-            here = pl.ds(pl.multiple_of(block * rows, rows), rows)
+        take(j, (2,), far)
+        for block in range(n):
+            here = slice(block * rows, (block + 1) * rows)
             query = near_sum[here, :] + jnp.dot(
                 q_all[here, pl.ds(distant, depth)], w_odd[j, pl.ds(distant, depth), :], preferred_element_type=jnp.float32
             )
-            query = (query * q_scale).astype(jnp.bfloat16)
-            top_logits(2 * j + 1, block, jnp.concatenate([query, pair_rope[here, :]], 1))
-            return carry
-
-        lax.fori_loop(0, n, odd_head, 0)
+            queries[here, 0:LANES] = (query * q_scale).astype(jnp.bfloat16)
+        for block in range(n):
+            top_logits(2 * j + 1, block, queries[block * rows : (block + 1) * rows, :])
+        return carry
+
+    lax.fori_loop(0, pairs, head_pair, 0)
 
     best = jnp.max(maxima[0:own, :], axis=1, keepdims=True)
     maxima[own : 2 * own, :] = jnp.broadcast_to(best, (own, maxima.shape[1]))
@@ -449,9 +451,10 @@
     kind = q_lat.dtype
     return pl.pallas_call(
         functools.partial(layer_kernel, n, m, own),
-        out_shape=jax.ShapeDtypeStruct((n, 2 * own, rows), jnp.float32),
+        out_shape=(pltpu.VMEM((n, 2 * own, rows), jnp.float32),)
+        + tuple(pltpu.VMEM(w.shape, w.dtype) for w in (w_nope, w_rope, w_kv)),
         in_specs=[any_ref] * 7,
-        out_specs=pl.BlockSpec(memory_space=pltpu.VMEM),
+        out_specs=(pl.BlockSpec(memory_space=pltpu.VMEM),) * 4,
         scratch_shapes=[
             pltpu.VMEM((tokens, m * q_lat.shape[1]), kind),
             pltpu.VMEM((tokens, m * kv_lat.shape[1]), kind),
@@ -463,27 +466,32 @@
             pltpu.VMEM((own, tokens, D_NOPE + LANES), kind),
             pltpu.VMEM((n, (REACH + 1) * rows, rows), jnp.float32),
             pltpu.VMEM((tokens, LANES), jnp.int32),
-            pltpu.VMEM((tokens, LANES), kind),
+            pltpu.VMEM((tokens, 2 * LANES), kind),
             pltpu.VMEM((tokens, LANES), jnp.float32),
             pltpu.VMEM((2 * own, tokens), jnp.float32),
             dma((moves,)), dma((n * m,)), dma((moves,)), dma((n * m,)), dma((moves,)), dma((n * m,)),
             dma((n,)), dma((n,)),
-            dma((parts * n,)), dma((parts * n,)), dma((n,)), dma((n,)), dma((4 + parts,)),
+            dma((parts * n,)), dma((parts * n,)), dma((n,)), dma((n,)), dma((7 + parts,)),
         ],
         compiler_params=pltpu.CompilerParams(
-            collective_id=0, has_side_effects=True, vmem_limit_bytes=44 * 1024 * 1024
+            collective_id=0, has_side_effects=True, vmem_limit_bytes=60 * 1024 * 1024
         ),
         name="layer",
-    )(q_lat, kv_lat, rope, segs, w_nope, w_rope, w_kv)
-
-
-def clip_kernel(n, own, got, threshold, w_nope, w_rope, w_kv, new_nope, new_rope, new_kv, head_max, row_max):
+    )(*(pltpu.with_memory_space_constraint(a, pltpu.HBM) for a in (q_lat, kv_lat, rope, segs, w_nope, w_rope, w_kv)))
+
+
+def clip_kernel(
+    n, own, got, threshold, w_nope, w_rope, w_kv, new_nope, new_rope, new_kv, head_max, row_max,
+    out_nope, out_rope, out_kv, sems,
+):
     limit = threshold[0]
     lane = lax.broadcasted_iota(jnp.int32, (1, LANES), 1)
     tops = jnp.zeros((1, head_max.shape[1]), jnp.float32)
     place = lax.broadcasted_iota(jnp.int32, tops.shape, 1)
-
-    def scaled(source, target, columns, factor):
+    copies = []
+
+    def scaled(source, target, column, factor):
+        columns = slice(column * LANES, (column + 1) * LANES)
         target[:, columns] = (source[:, columns].astype(jnp.float32) * factor).astype(target.dtype)
 
     for s in range(n):
@@ -492,43 +500,53 @@
         root = jnp.sqrt(clip)
         for i in range(own):
             head = s * own + i
-            columns = slice(head * LANES, (head + 1) * LANES)
-            scaled(w_nope, new_nope, columns, root[i : i + 1])
-            scaled(w_kv, new_kv, columns, root[i : i + 1])
+            scaled(w_nope, out_nope, head, root[i : i + 1])
+            scaled(w_kv, out_kv, head, root[i : i + 1])
             tops = jnp.where(place == head, top[i : i + 1, 0 : tops.shape[1]], tops)
         for j in range(own // 2):
-            pair = s * own // 2 + j
-            columns = slice(pair * LANES, (pair + 1) * LANES)
             factor = jnp.where(lane < D_ROPE, clip[2 * j : 2 * j + 1], clip[2 * j + 1 : 2 * j + 2])
-            scaled(w_rope, new_rope, columns, factor)
+            scaled(w_rope, out_rope, s * own // 2 + j, factor)
+        for i, (source, target) in enumerate(((out_nope, new_nope), (out_rope, new_rope), (out_kv, new_kv))):
+            width = source.shape[1] // n
+            at = pl.ds(s * width, width)
+            copy = pltpu.make_async_copy(source.at[:, at], target.at[:, at], sems.at[3 * s + i])
+            copy.start()
+            copies.append(copy)
         row_max[s * own : (s + 1) * own, :] = got[s, 0:own, :]
     head_max[...] = tops
+    for copy in copies:
+        copy.wait()
 
 
 def clip_weights(n, own, got, threshold, w_nope, w_rope, w_kv):
-    steps = 4 if w_nope.shape[0] % 64 == 0 and w_kv.shape[0] % 64 == 0 else 1
     weights = (w_nope, w_rope, w_kv)
-    blocks = [pl.BlockSpec((w.shape[0] // steps, w.shape[1]), lambda i: (i, 0)) for w in weights]
     heads = n * own
+    in_vmem = pl.BlockSpec(memory_space=pltpu.VMEM)
+    any_ref = pl.BlockSpec(memory_space=pl.ANY)
     return pl.pallas_call(
         functools.partial(clip_kernel, n, own),
-        grid=(steps,),
         out_shape=tuple(jax.ShapeDtypeStruct(w.shape, w.dtype) for w in weights)
         + (jax.ShapeDtypeStruct((1, heads), jnp.float32), jax.ShapeDtypeStruct((heads, got.shape[2]), jnp.float32)),
-        in_specs=[pl.BlockSpec(got.shape, lambda i: (0, 0, 0)), pl.BlockSpec(memory_space=pltpu.SMEM)] + blocks,
-        out_specs=tuple(blocks)
-        + (pl.BlockSpec((1, heads), lambda i: (0, 0)), pl.BlockSpec((heads, got.shape[2]), lambda i: (0, 0))),
-        compiler_params=pltpu.CompilerParams(dimension_semantics=("arbitrary",)),
+        in_specs=[in_vmem, pl.BlockSpec(memory_space=pltpu.SMEM)] + [in_vmem] * 3,
+        out_specs=(any_ref,) * 3 + (in_vmem,) * 2,
+        scratch_shapes=[pltpu.VMEM(w.shape, w.dtype) for w in weights] + [pltpu.SemaphoreType.DMA((3 * n,))],
+        compiler_params=pltpu.CompilerParams(vmem_limit_bytes=16 * 1024 * 1024),
         name="clip_weights",
-    )(got, threshold, w_nope, w_rope, w_kv)
+    )(
+        pltpu.with_memory_space_constraint(got, pltpu.VMEM),
+        threshold,
+        *(pltpu.with_memory_space_constraint(w, pltpu.VMEM) for w in weights),
+    )
 
 
 def owned_body(n, m, q_latent, kv_latent, k_rope, segment_ids, w_q_nope, w_q_rope, w_kv_nope, threshold):
     rows = q_latent.shape[0]
     heads = w_q_nope.shape[1] // D_NOPE
     own = heads // n
-    got = layer(n, m, own, q_latent, kv_latent, k_rope.T, segment_ids.reshape(1, rows), w_q_nope, w_q_rope, w_kv_nope)
-    new_nope, new_rope, new_kv, head_max, row_max = clip_weights(n, own, got, threshold, w_q_nope, w_q_rope, w_kv_nope)
+    got, *held = layer(
+        n, m, own, q_latent, kv_latent, k_rope.T, segment_ids.reshape(1, rows), w_q_nope, w_q_rope, w_kv_nope
+    )
+    new_nope, new_rope, new_kv, head_max, row_max = clip_weights(n, own, got, threshold, *held)
     return (new_nope, new_rope, new_kv, head_max.reshape(heads), row_max.T)
 
 

time: 112 us -> 94.7 us (0.85)
  Pallas kernels: 103 us -> 93.2 us
  local copies, waits for them, and re-layouts: 7.4 us -> 0 us
    pallas_call x2, Pallas kernels: 103 us -> 93.2 us  [the longest x1 90.8 us: layer(): pl.pallas_call(functools.partial(layer_kernel, n, m, own), out_shape=(plt...]
    unnamed x16 -> x0, local copies, waits for them, and re-layouts: 7.4 us -> none
where the time goes in v2:
time: 94.7 us; the launch traced here: 94.5 us
  Pallas kernels  93.2 us (98%)
  between operations  1.29 us (1%)
    pallas_call x1, Pallas kernels, layer(): pl.pallas_call(functools.partial(layer_kernel, n, m, own), out_shape=(plt...  90.8 us
    pallas_call x1, Pallas kernels, clip_weights(): pl.pallas_call(functools.partial(clip_kernel, n, own), out_shape=tuple((j...  2.46 us

profile of v2, /device:TPU:0, one launch (start us, length us, event | category | flops | bytes accessed | tf_op | source)
XLA Modules:
  0.0 94.5 jit_solution(11145063947740581636)
XLA Ops:
  1.3 90.8 %layer.1 = (f32[8,8,256]{2,1,0:T(8,128)S(1)}, bf16[192,4096]{1,0:T(8,128)(2,1)S(1)}, bf16[192,2048]{1,0:T(8,128)(2,1)S(1)}, bf16[64,4096]{1,0:T(8,128)(2,1)S(1)}) custom-call(bf16[256,384]{1,0:T(8,128)(2,1)} %q_lat.1, bf16[256,128]{1,0:T(8,128)(2,1)} %kv_lat.1, bf16[64,256]{1,0:T(8,128)(2,1)} %bitcast.4, s32[1,256]{1,0:T(1,128)} %bitcast.5, ...), custom_call_target="tpu_custom_call" | custom-call | tf_op jit(solution)/shard_map/layer/pallas_call | solution.py:452
  92.1 2.5 %clip_weights.1 = (bf16[192,4096]{1,0:T(8,128)(2,1)}, bf16[192,2048]{1,0:T(8,128)(2,1)}, bf16[64,4096]{1,0:T(8,128)(2,1)}, f32[1,32]{1,0:T(1,128)}, f32[32,256]{1,0:T(8,128)}) custom-call(f32[8,8,256]{2,1,0:T(8,128)S(1)} %get-tuple-element.14.got, f32[1]{0:T(128)S(6)} %copy.13.threshold, bf16[192,4096]{1,0:T(8,128)(2,1)S(1)} %get-tuple-element.15.w_nope, ...), custom_call_target="tpu_custom_call" | custom-call | tf_op jit(solution)/shard_map/clip_weights/pallas_call | solution.py:526

commit v3 on v2

--- a/solution.py
+++ b/solution.py
@@ -165,6 +165,7 @@
 
 MESH = pl.DeviceIdType.MESH
 LANES = 128
+EVEN_NOPE, PAIR_ROPE, ODD_NOPE, EVEN_KEY, ODD_KEY = KINDS = range(5)
 
 
 def other(index, stride):
@@ -185,9 +186,10 @@
 
 
 def layer_kernel(
-    n, m, own, q_lat, kv_lat, rope, segs, w_nope, w_rope, w_kv, got, held_nope, held_rope, held_kv,
-    q_all, kv_all, rope_all, segs_all, w_even, w_odd, w_key, keys, caps, seg_cols, queries, near_sum, maxima,
-    q_send, q_recv, kv_send, kv_recv, rope_send, rope_recv, seg_send, seg_recv, w_send, w_recv, max_send, max_recv, local,
+    n, m, own, q_lat, kv_lat, rope, segs, threshold, w_nope, w_rope, w_kv,
+    got_early, got_late, held_nope, held_rope, held_kv,
+    q_all, kv_all, rope_all, segs_all, w_even, w_odd, w_key, keys, caps, seg_cols, queries, near_sum, maxima, early, late,
+    q_send, q_recv, kv_send, kv_recv, rope_send, rope_recv, seg_send, seg_recv, w_send, w_recv, early_send, early_recv, late_send, late_recv, local,
 ):
     s = lax.axis_index("seq")
     h = lax.axis_index("head")
@@ -217,22 +219,25 @@
             rope_all.at[ps, pl.ds(pl.multiple_of(ph * part, part), part), :],
         )
 
+    def lanes(index, count=1):
+        return pl.ds(pl.multiple_of(index * LANES, LANES), count * LANES)
+
     def parts_of(p):
         found = []
         for j in range(pairs):
-            even = pl.ds(pl.multiple_of((p * own + 2 * j) * LANES, LANES), LANES)
-            odd = pl.ds(pl.multiple_of((p * own + 2 * j + 1) * LANES, LANES), LANES)
-            both = pl.ds(pl.multiple_of((p * pairs + j) * LANES, LANES), LANES)
-            found.append((w_nope.at[:, even], w_even, j, slice(0, LANES)))
-            found.append((w_rope.at[:, both], w_even, j, slice(LANES, 2 * LANES)))
-            found.append((w_nope.at[:, odd], w_odd, j, slice(0, LANES)))
-        found.append((w_kv.at[:, pl.ds(pl.multiple_of(p * own * LANES, LANES), own * LANES)], w_key, None, None))
+            found.append(w_nope.at[:, lanes(p * own + 2 * j)])
+            found.append(w_rope.at[:, lanes(p * pairs + j)])
+            found.append(w_nope.at[:, lanes(p * own + 2 * j + 1)])
+            found.append(w_kv.at[:, lanes(p * own + 2 * j)])
+            found.append(w_kv.at[:, lanes(p * own + 2 * j + 1)])
         return found
 
-    def landing(target, j, columns, source):
-        if j is None:
-            return target.at[pl.ds(pl.multiple_of(source * kv_rows, kv_rows), kv_rows), :]
-        return target.at[j, pl.ds(pl.multiple_of(source * q_rows, q_rows), q_rows), columns]
+    def landing(j, kind, source):
+        q_at = pl.ds(pl.multiple_of(source * q_rows, q_rows), q_rows)
+        kv_at = pl.ds(pl.multiple_of(source * kv_rows, kv_rows), kv_rows)
+        if kind < EVEN_KEY:
+            return (w_even.at[j, q_at, 0:LANES], w_even.at[j, q_at, LANES : 2 * LANES], w_odd.at[j, q_at, :])[kind]
+        return w_key.at[2 * j + kind - EVEN_KEY, kv_at, :]
 
     own_pieces = (q_lat, kv_lat, rope.at[pl.ds(pl.multiple_of(h * part, part), part), :], segs)
     loads = [
@@ -242,8 +247,8 @@
     for copy in loads:
         copy.start()
     keeps = [
-        pltpu.make_async_copy(src, landing(target, j, columns, s), local.at[4 + i])
-        for i, (src, target, j, columns) in enumerate(parts_of(s))
+        pltpu.make_async_copy(src, landing(i // len(KINDS), i % len(KINDS), s), local.at[4 + i])
+        for i, src in enumerate(parts_of(s))
     ] + [
         pltpu.make_async_copy(src, dst, local.at[4 + len(parts_of(s)) + i])
         for i, (src, dst) in enumerate(zip((w_nope, w_rope, w_kv), (held_nope, held_rope, held_kv)))
@@ -277,29 +282,30 @@
         for route in routes[reached + 1:]:
             push(k, g, route)
 
-    def weights(wanted, k):
+    def weights(j, wanted, k):
         p = flip(s, k)
-        for i, (src, target, j, columns) in enumerate(parts_of(p)):
-            if i in wanted:
-                copy = pltpu.make_async_remote_copy(
-                    src_ref=src, dst_ref=landing(target, j, columns, s),
-                    send_sem=w_send.at[i * n + k], recv_sem=w_recv.at[i * n + k],
-                    device_id=(p, h), device_id_type=MESH)
-                copy.start()
-                drains.append((src, w_send.at[i * n + k]))
+        sources = parts_of(p)
+        for kind in wanted:
+            i = j * len(KINDS) + kind
+            copy = pltpu.make_async_remote_copy(
+                src_ref=sources[i], dst_ref=landing(j, kind, s),
+                send_sem=w_send.at[i * n + k], recv_sem=w_recv.at[i * n + k],
+                device_id=(p, h), device_id_type=MESH)
+            copy.start()
+            drains.append((sources[i], w_send.at[i * n + k]))
 
     def take(j, wanted, ks):
         for k in ks:
-            for i in wanted:
-                target, columns = ((w_even, slice(0, LANES)), (w_even, slice(LANES, 2 * LANES)), (w_odd, slice(0, LANES)))[i]
-                ref = landing(target, j, columns, flip(s, k))
-                pltpu.make_async_copy(ref, ref, w_recv.at[(3 * j + i) * n + k]).wait()
+            for kind in wanted:
+                ref = landing(j, kind, flip(s, k))
+                pltpu.make_async_copy(ref, ref, w_recv.at[(j * len(KINDS) + kind) * n + k]).wait()
 
     far = [k ^ half for k in range(half)]
     near = list(range(half - 1, 0, -1))
-    kv_part = 3 * pairs
-    first = [0, 1]
-    later = [[kv_part]] + [[2]] + [group for j in range(1, pairs) for group in ([3 * j, 3 * j + 1], [3 * j + 2])]
+    first = (EVEN_NOPE, PAIR_ROPE)
+    later = [(0, (EVEN_KEY,)), (0, (ODD_NOPE,)), (0, (ODD_KEY,))]
+    for j in range(1, pairs):
+        later += [(j, first + (EVEN_KEY,)), (j, (ODD_NOPE,)), (j, (ODD_KEY,))]
 
     for route in routes:
         push(0, 0, route)
@@ -310,16 +316,16 @@
         copy.start()
         drains.append((segs_all.at[s], seg_send.at[k]))
     for k in far:
-        weights(first, k)
+        weights(0, first, k)
     order = sorted(range(1, n), key=lambda k: (bin(k).count("1"), k & 1 == 1 and bin(k).count("1") > 1, k))
     on_links = max(i for i, k in enumerate(order) if k & 1 == 0)
     for k in order[: on_links + 1]:
         relay(k, 0)
     for k in near:
-        weights(first, k)
-    for wanted in later:
+        weights(0, first, k)
+    for j, wanted in later:
         for k in far + near:
-            weights(wanted, k)
+            weights(j, wanted, k)
 
     for k in range(1, n):
         ref = segs_all.at[flip(s, k)]
@@ -356,105 +362,155 @@
 
     for copy in keeps:
         copy.wait()
-    for k in far + near:
-        ref = landing(w_key, None, None, flip(s, k))
-        pltpu.make_async_copy(ref, ref, w_recv.at[kv_part * n + k]).wait()
     q_scale = 1.0 / math.sqrt(QLORA)
     k_scale = 1.0 / math.sqrt(KVLORA)
     lane = lax.broadcasted_iota(jnp.int32, (rows, LANES), 1)
     sides = LANES // D_ROPE
-
-    def fill_keys(block, carry):
+    spare = rows // LANES
+
+    def fill_sides(block, carry):
         here = pl.ds(pl.multiple_of(block * rows, rows), rows)
-        key = (jnp.dot(kv_all[here, :], w_key[...], preferred_element_type=jnp.float32) * k_scale).astype(jnp.bfloat16)
         turned = jnp.concatenate([rope_all[block].astype(jnp.float32)] * sides, 0)
         twice = jnp.transpose(turned).astype(jnp.bfloat16)
         for i in range(own):
-            side = jnp.where(lane // D_ROPE == i % sides, twice, jnp.zeros_like(twice))
-            keys[i, here, :] = jnp.concatenate([key[:, i * D_NOPE : (i + 1) * D_NOPE], side], 1)
+            keys[i, here, LANES : 2 * LANES] = jnp.where(lane // D_ROPE == i % sides, twice, jnp.zeros_like(twice))
         return carry
 
-    lax.fori_loop(0, n, fill_keys, 0)
-
-    def top_logits(i, block, q_head):
+    lax.fori_loop(0, n, fill_sides, 0)
+    maxima[...] = jnp.zeros_like(maxima)
+
+    def span(block):
+        return slice(block * rows, (block + 1) * rows)
+
+    def top_logits(i, block):
         first = max(block - REACH, 0)
         best = None
         for other_block in range(first, block + 1):
             logits = lax.dot_general(
-                keys[i, other_block * rows : (other_block + 1) * rows, :], q_head,
+                keys[i, span(other_block), :], queries[span(block), :],
                 (((1,), (1,)), ((), ())), preferred_element_type=jnp.float32,
             )
-            cap = caps[block, (other_block - first) * rows : (other_block - first + 1) * rows, :]
+            cap = caps[block, span(other_block - first), :]
             top = jnp.max(jnp.minimum(logits, cap).reshape(rows // 8, 8, rows), axis=0)
             best = top if best is None else jnp.maximum(best, top)
         top = jnp.max(best, axis=0, keepdims=True) * (1.0 / math.sqrt(D_NOPE + D_ROPE))
-        maxima[pl.ds(i, 1), block * rows : (block + 1) * rows] = top
-
-    depth = half * q_rows
+        maxima[pl.ds(i, 1), span(block)] = top
+        return top
+
+    depth = half * kv_rows
     close = pl.multiple_of(s // half * depth, depth)
     distant = pl.multiple_of((1 - s // half) * depth, depth)
 
+    def share_early():
+        early[0:own, :] = maxima[...]
+        early[own : 2 * own, :] = jnp.broadcast_to(jnp.max(maxima[...], axis=1, keepdims=True), maxima.shape)
+        for k in range(1, n):
+            p = flip(s, k)
+            pltpu.make_async_remote_copy(
+                src_ref=early.at[:, pl.ds(pl.multiple_of(p * rows, rows), rows)], dst_ref=got_early.at[s],
+                send_sem=early_send.at[k], recv_sem=early_recv.at[k], device_id=(p, h), device_id_type=MESH).start()
+        got_early[s] = early[:, pl.ds(pl.multiple_of(s * rows, rows), rows)]
+
+    def scale_early():
+        for k in range(1, n):
+            gone = early.at[:, pl.ds(pl.multiple_of(flip(s, k) * rows, rows), rows)]
+            pltpu.make_async_copy(gone, gone, early_send.at[k]).wait()
+            come = got_early.at[flip(s, k)]
+            pltpu.make_async_copy(come, come, early_recv.at[k]).wait()
+        for p in range(n):
+            clip = clip_of(got_early[p, own : 2 * own, 0:LANES], threshold[0])
+            root = jnp.sqrt(clip)
+            for i in range(own - 1):
+                at = slice((p * own + i) * LANES, (p * own + i + 1) * LANES)
+                scale_columns(held_nope, at, held_nope, at, root[i : i + 1])
+                scale_columns(held_kv, at, held_kv, at, root[i : i + 1])
+            for j in range(pairs):
+                at = slice((p * pairs + j) * LANES, (p * pairs + j + 1) * LANES)
+                odd = clip[2 * j + 1 : 2 * j + 2] if j < pairs - 1 else jnp.ones((1, LANES), jnp.float32)
+                factor = jnp.where(lane[0:1] < D_ROPE, clip[2 * j : 2 * j + 1], odd)
+                scale_columns(held_rope, at, held_rope, at, factor)
+
     def head_pair(j, carry):
-        take(j, (0, 1), far + near)
-        for block in range(n):
-            here = slice(block * rows, (block + 1) * rows)
-            query = jnp.dot(q_all[here, :], w_even[j], preferred_element_type=jnp.float32)
-            queries[here, :] = (query * q_scale).astype(jnp.bfloat16)
-        for block in range(n):
-            top_logits(2 * j, block, queries[block * rows : (block + 1) * rows, :])
-        take(j, (2,), near)
-        for block in range(n):
-            here = slice(block * rows, (block + 1) * rows)
-            near_sum[here, :] = jnp.dot(
-                q_all[here, pl.ds(close, depth)], w_odd[j, pl.ds(close, depth), :], preferred_element_type=jnp.float32
+        take(j, (EVEN_KEY,), far + near)
+        for block in range(n):
+            key = jnp.dot(kv_all[span(block), :], w_key[2 * j], preferred_element_type=jnp.float32)
+            keys[2 * j, span(block), 0:LANES] = (key * k_scale).astype(jnp.bfloat16)
+        take(j, first, far + near)
+        for block in range(n):
+            query = jnp.dot(q_all[span(block), :], w_even[j], preferred_element_type=jnp.float32)
+            queries[span(block), :] = (query * q_scale).astype(jnp.bfloat16)
+        for block in range(n):
+            top_logits(2 * j, block)
+        pl.when(j == pairs - 1)(share_early)
+        take(j, (ODD_NOPE,), far + near)
+        for block in range(n):
+            query = jnp.dot(q_all[span(block), :], w_odd[j], preferred_element_type=jnp.float32)
+            queries[span(block), 0:LANES] = (query * q_scale).astype(jnp.bfloat16)
+        take(j, (ODD_KEY,), near)
+        for block in range(n):
+            near_sum[span(block), :] = jnp.dot(
+                kv_all[span(block), pl.ds(close, depth)], w_key[2 * j + 1, pl.ds(close, depth), :],
+                preferred_element_type=jnp.float32,
             )
-        take(j, (2,), far)
-        for block in range(n):
-            here = slice(block * rows, (block + 1) * rows)
-            query = near_sum[here, :] + jnp.dot(
-                q_all[here, pl.ds(distant, depth)], w_odd[j, pl.ds(distant, depth), :], preferred_element_type=jnp.float32
+        pl.when(j == pairs - 1)(scale_early)
+        take(j, (ODD_KEY,), far)
+        for block in range(n):
+            key = near_sum[span(block), :] + jnp.dot(
+                kv_all[span(block), pl.ds(distant, depth)], w_key[2 * j + 1, pl.ds(distant, depth), :],
+                preferred_element_type=jnp.float32,
             )
-            queries[here, 0:LANES] = (query * q_scale).astype(jnp.bfloat16)
-        for block in range(n):
-            top_logits(2 * j + 1, block, queries[block * rows : (block + 1) * rows, :])
+            keys[2 * j + 1, span(block), 0:LANES] = (key * k_scale).astype(jnp.bfloat16)
+        best = None
+        for block in range(n):
+            top = top_logits(2 * j + 1, block)
+            for c in range(spare):
+                late[block, c : c + 1, :] = top[:, c * LANES : (c + 1) * LANES]
+            best = top if best is None else jnp.maximum(best, top)
+        best = jnp.broadcast_to(jnp.max(best, axis=1, keepdims=True), (late.shape[1] - spare, LANES))
+        for block in range(n):
+            late[block, spare : late.shape[1], :] = best
         return carry
 
     lax.fori_loop(0, pairs, head_pair, 0)
 
-    best = jnp.max(maxima[0:own, :], axis=1, keepdims=True)
-    maxima[own : 2 * own, :] = jnp.broadcast_to(best, (own, maxima.shape[1]))
-    shares = []
     for k in range(1, n):
         p = flip(s, k)
-        copy = pltpu.make_async_remote_copy(
-            src_ref=maxima.at[:, pl.ds(pl.multiple_of(p * rows, rows), rows)], dst_ref=got.at[s],
-            send_sem=max_send.at[k], recv_sem=max_recv.at[k], device_id=(p, h), device_id_type=MESH)
-        copy.start()
-        shares.append(copy)
-    got[s] = maxima[:, pl.ds(pl.multiple_of(s * rows, rows), rows)]
+        pltpu.make_async_remote_copy(
+            src_ref=late.at[p], dst_ref=got_late.at[s], send_sem=late_send.at[k], recv_sem=late_recv.at[k],
+            device_id=(p, h), device_id_type=MESH).start()
+        drains.append((late.at[p], late_send.at[k]))
+    got_late[s] = late[s]
     for ref, sent in drains:
         pltpu.make_async_copy(ref, ref, sent).wait()
-    for k, copy in zip(range(1, n), shares):
-        copy.wait_send()
-        at = got.at[flip(s, k)]
-        pltpu.make_async_copy(at, at, max_recv.at[k]).wait()
-
-
-def layer(n, m, own, q_lat, kv_lat, rope, segs, w_nope, w_rope, w_kv):
+    for k in range(1, n):
+        come = got_late.at[flip(s, k)]
+        pltpu.make_async_copy(come, come, late_recv.at[k]).wait()
+
+
+def clip_of(top, limit):
+    return limit / jnp.maximum(top, limit)
+
+
+def scale_columns(source, columns, target, at, factor):
+    target[:, at] = (source[:, columns].astype(jnp.float32) * factor).astype(target.dtype)
+
+
+def layer(n, m, own, q_lat, kv_lat, rope, segs, threshold, w_nope, w_rope, w_kv):
     rows = q_lat.shape[0]
     tokens = n * rows
     pairs = own // 2
     moves = n * m - 1
-    parts = 3 * pairs + 1
+    parts = len(KINDS) * pairs
+    late = rows // LANES + 2
     any_ref = pl.BlockSpec(memory_space=pl.ANY)
     dma = pltpu.SemaphoreType.DMA
     kind = q_lat.dtype
     return pl.pallas_call(
         functools.partial(layer_kernel, n, m, own),
-        out_shape=(pltpu.VMEM((n, 2 * own, rows), jnp.float32),)
+        out_shape=(pltpu.VMEM((n, 2 * own, rows), jnp.float32), pltpu.VMEM((n, late, LANES), jnp.float32))
         + tuple(pltpu.VMEM(w.shape, w.dtype) for w in (w_nope, w_rope, w_kv)),
-        in_specs=[any_ref] * 7,
-        out_specs=(pl.BlockSpec(memory_space=pltpu.VMEM),) * 4,
+        in_specs=[any_ref] * 4 + [pl.BlockSpec(memory_space=pltpu.SMEM)] + [any_ref] * 3,
+        out_specs=(pl.BlockSpec(memory_space=pltpu.VMEM),) * 5,
         scratch_shapes=[
             pltpu.VMEM((tokens, m * q_lat.shape[1]), kind),
             pltpu.VMEM((tokens, m * kv_lat.shape[1]), kind),
@@ -462,78 +518,90 @@
             pltpu.VMEM((n,) + segs.shape, jnp.int32),
             pltpu.VMEM((pairs, n * w_nope.shape[0], 2 * LANES), kind),
             pltpu.VMEM((pairs, n * w_nope.shape[0], LANES), kind),
-            pltpu.VMEM((n * w_kv.shape[0], own * LANES), kind),
+            pltpu.VMEM((own, n * w_kv.shape[0], LANES), kind),
             pltpu.VMEM((own, tokens, D_NOPE + LANES), kind),
             pltpu.VMEM((n, (REACH + 1) * rows, rows), jnp.float32),
             pltpu.VMEM((tokens, LANES), jnp.int32),
             pltpu.VMEM((tokens, 2 * LANES), kind),
             pltpu.VMEM((tokens, LANES), jnp.float32),
+            pltpu.VMEM((own, tokens), jnp.float32),
             pltpu.VMEM((2 * own, tokens), jnp.float32),
+            pltpu.VMEM((n, late, LANES), jnp.float32),
             dma((moves,)), dma((n * m,)), dma((moves,)), dma((n * m,)), dma((moves,)), dma((n * m,)),
             dma((n,)), dma((n,)),
-            dma((parts * n,)), dma((parts * n,)), dma((n,)), dma((n,)), dma((7 + parts,)),
+            dma((parts * n,)), dma((parts * n,)), dma((n,)), dma((n,)), dma((n,)), dma((n,)), dma((7 + parts,)),
         ],
         compiler_params=pltpu.CompilerParams(
             collective_id=0, has_side_effects=True, vmem_limit_bytes=60 * 1024 * 1024
         ),
         name="layer",
-    )(*(pltpu.with_memory_space_constraint(a, pltpu.HBM) for a in (q_lat, kv_lat, rope, segs, w_nope, w_rope, w_kv)))
+    )(
+        *(pltpu.with_memory_space_constraint(a, pltpu.HBM) for a in (q_lat, kv_lat, rope, segs)),
+        threshold,
+        *(pltpu.with_memory_space_constraint(w, pltpu.HBM) for w in (w_nope, w_rope, w_kv)),
+    )
 
 
 def clip_kernel(
-    n, own, got, threshold, w_nope, w_rope, w_kv, new_nope, new_rope, new_kv, head_max, row_max,
-    out_nope, out_rope, out_kv, sems,
+    n, own, got_early, got_late, threshold, w_nope, w_rope, w_kv, new_nope, new_rope, new_kv, head_max, row_max,
+    last_nope, last_rope, last_kv, sems,
 ):
-    limit = threshold[0]
     lane = lax.broadcasted_iota(jnp.int32, (1, LANES), 1)
     tops = jnp.zeros((1, head_max.shape[1]), jnp.float32)
     place = lax.broadcasted_iota(jnp.int32, tops.shape, 1)
+    groups = ((w_nope, last_nope, new_nope, own), (w_rope, last_rope, new_rope, own // 2), (w_kv, last_kv, new_kv, own))
     copies = []
 
-    def scaled(source, target, column, factor):
-        columns = slice(column * LANES, (column + 1) * LANES)
-        target[:, columns] = (source[:, columns].astype(jnp.float32) * factor).astype(target.dtype)
+    def put(source, columns, target, at):
+        copy = pltpu.make_async_copy(source.at[:, columns], target.at[:, at], sems.at[len(copies)])
+        copy.start()
+        copies.append(copy)
 
     for s in range(n):
-        top = got[s, own : 2 * own, 0:LANES]
-        clip = limit / jnp.maximum(top, limit)
+        for whole, _, target, count in groups:
+            ready = pl.ds(s * count * LANES, (count - 1) * LANES)
+            put(whole, ready, target, ready)
+    for s in range(n):
+        spare = row_max.shape[1] // LANES
+        clip = clip_of(got_late[s, spare : spare + 1, :], threshold[0])
         root = jnp.sqrt(clip)
-        for i in range(own):
-            head = s * own + i
-            scaled(w_nope, out_nope, head, root[i : i + 1])
-            scaled(w_kv, out_kv, head, root[i : i + 1])
-            tops = jnp.where(place == head, top[i : i + 1, 0 : tops.shape[1]], tops)
-        for j in range(own // 2):
-            factor = jnp.where(lane < D_ROPE, clip[2 * j : 2 * j + 1], clip[2 * j + 1 : 2 * j + 2])
-            scaled(w_rope, out_rope, s * own // 2 + j, factor)
-        for i, (source, target) in enumerate(((out_nope, new_nope), (out_rope, new_rope), (out_kv, new_kv))):
-            width = source.shape[1] // n
-            at = pl.ds(s * width, width)
-            copy = pltpu.make_async_copy(source.at[:, at], target.at[:, at], sems.at[3 * s + i])
-            copy.start()
-            copies.append(copy)
-        row_max[s * own : (s + 1) * own, :] = got[s, 0:own, :]
+        mine = slice(s * LANES, (s + 1) * LANES)
+        factors = (root, jnp.where(lane < D_ROPE, 1.0, clip), root)
+        for (whole, last, target, count), factor in zip(groups, factors):
+            at = slice(((s + 1) * count - 1) * LANES, (s + 1) * count * LANES)
+            scale_columns(whole, at, last, mine, factor)
+            put(last, pl.ds(s * LANES, LANES), target, pl.ds(((s + 1) * count - 1) * LANES, LANES))
+    for s in range(n):
+        early = got_early[s, own : 2 * own, 0 : tops.shape[1]]
+        for i in range(own - 1):
+            tops = jnp.where(place == s * own + i, early[i : i + 1], tops)
+        tops = jnp.where(place == s * own + own - 1, got_late[s, spare : spare + 1, 0 : tops.shape[1]], tops)
+        row_max[s * own : (s + 1) * own - 1, :] = got_early[s, 0 : own - 1, :]
+        for c in range(spare):
+            row_max[(s + 1) * own - 1 : (s + 1) * own, c * LANES : (c + 1) * LANES] = got_late[s, c : c + 1, :]
     head_max[...] = tops
     for copy in copies:
         copy.wait()
 
 
-def clip_weights(n, own, got, threshold, w_nope, w_rope, w_kv):
+def clip_weights(n, own, got_early, got_late, threshold, w_nope, w_rope, w_kv):
     weights = (w_nope, w_rope, w_kv)
     heads = n * own
     in_vmem = pl.BlockSpec(memory_space=pltpu.VMEM)
     any_ref = pl.BlockSpec(memory_space=pl.ANY)
+    rows = got_early.shape[2]
     return pl.pallas_call(
         functools.partial(clip_kernel, n, own),
         out_shape=tuple(jax.ShapeDtypeStruct(w.shape, w.dtype) for w in weights)
-        + (jax.ShapeDtypeStruct((1, heads), jnp.float32), jax.ShapeDtypeStruct((heads, got.shape[2]), jnp.float32)),
-        in_specs=[in_vmem, pl.BlockSpec(memory_space=pltpu.SMEM)] + [in_vmem] * 3,
+        + (jax.ShapeDtypeStruct((1, heads), jnp.float32), jax.ShapeDtypeStruct((heads, rows), jnp.float32)),
+        in_specs=[in_vmem] * 2 + [pl.BlockSpec(memory_space=pltpu.SMEM)] + [in_vmem] * 3,
         out_specs=(any_ref,) * 3 + (in_vmem,) * 2,
-        scratch_shapes=[pltpu.VMEM(w.shape, w.dtype) for w in weights] + [pltpu.SemaphoreType.DMA((3 * n,))],
+        scratch_shapes=[pltpu.VMEM((w.shape[0], n * LANES), w.dtype) for w in weights]
+        + [pltpu.SemaphoreType.DMA((6 * n,))],
         compiler_params=pltpu.CompilerParams(vmem_limit_bytes=16 * 1024 * 1024),
         name="clip_weights",
     )(
-        pltpu.with_memory_space_constraint(got, pltpu.VMEM),
+        *(pltpu.with_memory_space_constraint(g, pltpu.VMEM) for g in (got_early, got_late)),
         threshold,
         *(pltpu.with_memory_space_constraint(w, pltpu.VMEM) for w in weights),
     )
@@ -543,10 +611,10 @@
     rows = q_latent.shape[0]
     heads = w_q_nope.shape[1] // D_NOPE
     own = heads // n
-    got, *held = layer(
-        n, m, own, q_latent, kv_latent, k_rope.T, segment_ids.reshape(1, rows), w_q_nope, w_q_rope, w_kv_nope
-    )
-    new_nope, new_rope, new_kv, head_max, row_max = clip_weights(n, own, got, threshold, *held)
+    got_early, got_late, *held = layer(
+        n, m, own, q_latent, kv_latent, k_rope.T, segment_ids.reshape(1, rows), threshold, w_q_nope, w_q_rope, w_kv_nope
+    )
+    new_nope, new_rope, new_kv, head_max, row_max = clip_weights(n, own, got_early, got_late, threshold, *held)
     return (new_nope, new_rope, new_kv, head_max.reshape(heads), row_max.T)
 
 

time: 94.7 us -> 97.9 us (1.034)
  Pallas kernels: 93.2 us -> 96.4 us
    pallas_call x1, Pallas kernels: 90.8 us -> 93.9 us  [layer(): pl.pallas_call(functools.partial(layer_kernel, n, m, own), out_shape=(plt...]
where the time goes in v3:
time: 97.9 us; the launch traced here: 97.7 us
  Pallas kernels  96.4 us (98%)
  between operations  1.29 us (1%)
    pallas_call x1, Pallas kernels, layer(): pl.pallas_call(functools.partial(layer_kernel, n, m, own), out_shape=(plt...  93.9 us
    pallas_call x1, Pallas kernels, clip_weights(): pl.pallas_call(functools.partial(clip_kernel, n, own), out_shape=tuple((j...  2.59 us

profile of v3, /device:TPU:0, one launch (start us, length us, event | category | flops | bytes accessed | tf_op | source)
XLA Modules:
  0.0 97.7 jit_solution(12556870220096248943)
XLA Ops:
  1.3 93.9 %layer.1 = (f32[8,8,256]{2,1,0:T(8,128)S(1)}, f32[8,4,128]{2,1,0:T(4,128)S(1)}, bf16[192,4096]{1,0:T(8,128)(2,1)S(1)}, bf16[192,2048]{1,0:T(8,128)(2,1)S(1)}, bf16[64,4096]{1,0:T(8,128)(2,1)S(1)}) custom-call(bf16[256,384]{1,0:T(8,128)(2,1)} %q_lat.1, bf16[256,128]{1,0:T(8,128)(2,1)} %kv_lat.1, bf16[64,256]{1,0:T(8,128)(2,1)} %bitcast.4, s32[1,256]{1,0:T(1,128)} %bitcast.5, ...), custom_call_target="tpu_custom_call" | custom-call | tf_op jit(solution)/shard_map/layer/pallas_call | solution.py:508
  95.1 2.6 %clip_weights.1 = (bf16[192,4096]{1,0:T(8,128)(2,1)}, bf16[192,2048]{1,0:T(8,128)(2,1)}, bf16[64,4096]{1,0:T(8,128)(2,1)}, f32[1,32]{1,0:T(1,128)}, f32[32,256]{1,0:T(8,128)}) custom-call(f32[8,8,256]{2,1,0:T(8,128)S(1)} %get-tuple-element.15.got_early, f32[8,4,128]{2,1,0:T(4,128)S(1)} %get-tuple-element.16.got_late, f32[1]{0:T(128)S(6)} %copy.13.threshold, ...), custom_call_target="tpu_custom_call" | custom-call | tf_op jit(solution)/shard_map/clip_weights/pallas_call | solution.py:593

commit v4 on v2

--- a/solution.py
+++ b/solution.py
@@ -165,6 +165,7 @@
 
 MESH = pl.DeviceIdType.MESH
 LANES = 128
+ROPE, KEY, GROUP, SINGLE, FINAL = KINDS = range(5)
 
 
 def other(index, stride):
@@ -185,8 +186,9 @@
 
 
 def layer_kernel(
-    n, m, own, q_lat, kv_lat, rope, segs, w_nope, w_rope, w_kv, got, held_nope, held_rope, held_kv,
-    q_all, kv_all, rope_all, segs_all, w_even, w_odd, w_key, keys, caps, seg_cols, queries, near_sum, maxima,
+    n, m, own, q_lat, kv_lat, rope, segs, w_nope, w_rope, w_kv,
+    got, held_nope, held_rope, held_kv,
+    q_all, kv_all, rope_all, segs_all, w_pos, w_key, w_group, w_lone, keys, caps, seg_cols, q_pos, q_nope, near_query, maxima,
     q_send, q_recv, kv_send, kv_recv, rope_send, rope_recv, seg_send, seg_recv, w_send, w_recv, max_send, max_recv, local,
 ):
     s = lax.axis_index("seq")
@@ -215,35 +217,38 @@
             window(q_all, q_lat.shape[1], ps, ph),
             window(kv_all, kv_lat.shape[1], ps, ph),
             rope_all.at[ps, pl.ds(pl.multiple_of(ph * part, part), part), :],
-        )
+            segs_all.at[ps],
+        )
+
+    def lanes(index, count=1):
+        return pl.ds(pl.multiple_of(index * LANES, LANES), count * LANES)
 
     def parts_of(p):
-        found = []
-        for j in range(pairs):
-            even = pl.ds(pl.multiple_of((p * own + 2 * j) * LANES, LANES), LANES)
-            odd = pl.ds(pl.multiple_of((p * own + 2 * j + 1) * LANES, LANES), LANES)
-            both = pl.ds(pl.multiple_of((p * pairs + j) * LANES, LANES), LANES)
-            found.append((w_nope.at[:, even], w_even, j, slice(0, LANES)))
-            found.append((w_rope.at[:, both], w_even, j, slice(LANES, 2 * LANES)))
-            found.append((w_nope.at[:, odd], w_odd, j, slice(0, LANES)))
-        found.append((w_kv.at[:, pl.ds(pl.multiple_of(p * own * LANES, LANES), own * LANES)], w_key, None, None))
-        return found
-
-    def landing(target, j, columns, source):
-        if j is None:
-            return target.at[pl.ds(pl.multiple_of(source * kv_rows, kv_rows), kv_rows), :]
-        return target.at[j, pl.ds(pl.multiple_of(source * q_rows, q_rows), q_rows), columns]
+        return (
+            w_rope.at[:, lanes(p * pairs, pairs)],
+            w_kv.at[:, lanes(p * own, own)],
+            w_nope.at[:, lanes(p * own, own - 2)],
+            w_nope.at[:, lanes(p * own + own - 2)],
+            w_nope.at[:, lanes(p * own + own - 1)],
+        )
+
+    def landing(kind, source):
+        q_at = pl.ds(pl.multiple_of(source * q_rows, q_rows), q_rows)
+        kv_at = pl.ds(pl.multiple_of(source * kv_rows, kv_rows), kv_rows)
+        return (
+            w_pos.at[q_at, :], w_key.at[kv_at, :], w_group.at[q_at, :], w_lone.at[0, q_at, :], w_lone.at[1, q_at, :]
+        )[kind]
 
     own_pieces = (q_lat, kv_lat, rope.at[pl.ds(pl.multiple_of(h * part, part), part), :], segs)
     loads = [
         pltpu.make_async_copy(src, dst, local.at[i])
-        for i, (src, dst) in enumerate(zip(own_pieces, places(0, 0) + (segs_all.at[s],)))
+        for i, (src, dst) in enumerate(zip(own_pieces, places(0, 0)))
     ]
     for copy in loads:
         copy.start()
     keeps = [
-        pltpu.make_async_copy(src, landing(target, j, columns, s), local.at[4 + i])
-        for i, (src, target, j, columns) in enumerate(parts_of(s))
+        pltpu.make_async_copy(src, landing(i, s), local.at[4 + i])
+        for i, src in enumerate(parts_of(s))
     ] + [
         pltpu.make_async_copy(src, dst, local.at[4 + len(parts_of(s)) + i])
         for i, (src, dst) in enumerate(zip((w_nope, w_rope, w_kv), (held_nope, held_rope, held_kv)))
@@ -256,6 +261,8 @@
 
     drains = []
     slots = [0]
+    sends = (q_send, kv_send, rope_send, seg_send)
+    recvs = (q_recv, kv_recv, rope_recv, seg_recv)
 
     def push(k, g, route):
         axis, stride = route
@@ -263,7 +270,8 @@
         at = (k ^ stride) * m + g if axis == "seq" else k * m + (g ^ stride)
         slot = slots[0]
         slots[0] += 1
-        for ref, sent, taken in zip(places(k, g), (q_send, kv_send, rope_send), (q_recv, kv_recv, rope_recv)):
+        count = 4 if axis == "seq" else 3
+        for ref, sent, taken in zip(places(k, g)[:count], sends, recvs):
             copy = pltpu.make_async_remote_copy(
                 src_ref=ref, dst_ref=ref, send_sem=sent.at[slot], recv_sem=taken.at[at],
                 device_id=target, device_id_type=MESH)
@@ -271,59 +279,45 @@
             drains.append((ref, sent.at[slot]))
 
     def relay(k, g):
-        for ref, taken in zip(places(k, g), (q_recv, kv_recv, rope_recv)):
+        for ref, taken in zip(places(k, g)[: 4 if g == 0 else 3], recvs):
             pltpu.make_async_copy(ref, ref, taken.at[k * m + g]).wait()
         reached = max(i for i, (axis, stride) in enumerate(routes) if (k if axis == "seq" else g) & stride)
         for route in routes[reached + 1:]:
             push(k, g, route)
 
-    def weights(wanted, k):
+    def weights(kind, k):
         p = flip(s, k)
-        for i, (src, target, j, columns) in enumerate(parts_of(p)):
-            if i in wanted:
-                copy = pltpu.make_async_remote_copy(
-                    src_ref=src, dst_ref=landing(target, j, columns, s),
-                    send_sem=w_send.at[i * n + k], recv_sem=w_recv.at[i * n + k],
-                    device_id=(p, h), device_id_type=MESH)
-                copy.start()
-                drains.append((src, w_send.at[i * n + k]))
-
-    def take(j, wanted, ks):
+        source = parts_of(p)[kind]
+        copy = pltpu.make_async_remote_copy(
+            src_ref=source, dst_ref=landing(kind, s),
+            send_sem=w_send.at[kind * n + k], recv_sem=w_recv.at[kind * n + k],
+            device_id=(p, h), device_id_type=MESH)
+        copy.start()
+        drains.append((source, w_send.at[kind * n + k]))
+
+    def take(kind, ks):
         for k in ks:
-            for i in wanted:
-                target, columns = ((w_even, slice(0, LANES)), (w_even, slice(LANES, 2 * LANES)), (w_odd, slice(0, LANES)))[i]
-                ref = landing(target, j, columns, flip(s, k))
-                pltpu.make_async_copy(ref, ref, w_recv.at[(3 * j + i) * n + k]).wait()
+            ref = landing(kind, flip(s, k))
+            pltpu.make_async_copy(ref, ref, w_recv.at[kind * n + k]).wait()
 
     far = [k ^ half for k in range(half)]
     near = list(range(half - 1, 0, -1))
-    kv_part = 3 * pairs
-    first = [0, 1]
-    later = [[kv_part]] + [[2]] + [group for j in range(1, pairs) for group in ([3 * j, 3 * j + 1], [3 * j + 2])]
 
     for route in routes:
         push(0, 0, route)
-    for k in range(1, n):
-        copy = pltpu.make_async_remote_copy(
-            src_ref=segs_all.at[s], dst_ref=segs_all.at[s], send_sem=seg_send.at[k], recv_sem=seg_recv.at[k],
-            device_id=(flip(s, k), h), device_id_type=MESH)
-        copy.start()
-        drains.append((segs_all.at[s], seg_send.at[k]))
     for k in far:
-        weights(first, k)
+        weights(ROPE, k)
     order = sorted(range(1, n), key=lambda k: (bin(k).count("1"), k & 1 == 1 and bin(k).count("1") > 1, k))
     on_links = max(i for i, k in enumerate(order) if k & 1 == 0)
     for k in order[: on_links + 1]:
         relay(k, 0)
     for k in near:
-        weights(first, k)
-    for wanted in later:
+        weights(ROPE, k)
+    for kind in KINDS[1:]:
         for k in far + near:
-            weights(wanted, k)
-
-    for k in range(1, n):
-        ref = segs_all.at[flip(s, k)]
-        pltpu.make_async_copy(ref, ref, seg_recv.at[k]).wait()
+            weights(kind, k)
+    for k in order[on_links + 1 :]:
+        relay(k, 0)
 
     def fill_segs(block, carry):
         here = pl.ds(pl.multiple_of(block * rows, rows), rows)
@@ -348,96 +342,109 @@
 
     lax.fori_loop(0, n, fill_caps, 0)
 
-    for k in order[on_links + 1:]:
-        relay(k, 0)
     for g in range(1, m):
         for k in [0] + order:
             relay(k, g)
 
     for copy in keeps:
         copy.wait()
-    for k in far + near:
-        ref = landing(w_key, None, None, flip(s, k))
-        pltpu.make_async_copy(ref, ref, w_recv.at[kv_part * n + k]).wait()
     q_scale = 1.0 / math.sqrt(QLORA)
     k_scale = 1.0 / math.sqrt(KVLORA)
     lane = lax.broadcasted_iota(jnp.int32, (rows, LANES), 1)
     sides = LANES // D_ROPE
 
-    def fill_keys(block, carry):
+    def fill_sides(block, carry):
         here = pl.ds(pl.multiple_of(block * rows, rows), rows)
-        key = (jnp.dot(kv_all[here, :], w_key[...], preferred_element_type=jnp.float32) * k_scale).astype(jnp.bfloat16)
         turned = jnp.concatenate([rope_all[block].astype(jnp.float32)] * sides, 0)
         twice = jnp.transpose(turned).astype(jnp.bfloat16)
         for i in range(own):
-            side = jnp.where(lane // D_ROPE == i % sides, twice, jnp.zeros_like(twice))
-            keys[i, here, :] = jnp.concatenate([key[:, i * D_NOPE : (i + 1) * D_NOPE], side], 1)
+            keys[i, here, LANES : 2 * LANES] = jnp.where(lane // D_ROPE == i % sides, twice, jnp.zeros_like(twice))
         return carry
 
-    lax.fori_loop(0, n, fill_keys, 0)
-
-    def top_logits(i, block, q_head):
+    lax.fori_loop(0, n, fill_sides, 0)
+
+    def span(block):
+        return slice(block * rows, (block + 1) * rows)
+
+    def top_logits(i, block):
         first = max(block - REACH, 0)
+        query = jnp.concatenate([q_nope[i, span(block), :], q_pos[span(block), i // sides * LANES : (i // sides + 1) * LANES]], 1)
         best = None
         for other_block in range(first, block + 1):
             logits = lax.dot_general(
-                keys[i, other_block * rows : (other_block + 1) * rows, :], q_head,
-                (((1,), (1,)), ((), ())), preferred_element_type=jnp.float32,
+                keys[i, span(other_block), :], query, (((1,), (1,)), ((), ())), preferred_element_type=jnp.float32
             )
-            cap = caps[block, (other_block - first) * rows : (other_block - first + 1) * rows, :]
+            cap = caps[block, span(other_block - first), :]
             top = jnp.max(jnp.minimum(logits, cap).reshape(rows // 8, 8, rows), axis=0)
             best = top if best is None else jnp.maximum(best, top)
         top = jnp.max(best, axis=0, keepdims=True) * (1.0 / math.sqrt(D_NOPE + D_ROPE))
-        maxima[pl.ds(i, 1), block * rows : (block + 1) * rows] = top
-
-    depth = half * q_rows
-    close = pl.multiple_of(s // half * depth, depth)
-    distant = pl.multiple_of((1 - s // half) * depth, depth)
-
-    def head_pair(j, carry):
-        take(j, (0, 1), far + near)
+        maxima[block, i : i + 1, 0:rows] = top
+        return top
+
+    def head_logits(i):
+        best = None
         for block in range(n):
-            here = slice(block * rows, (block + 1) * rows)
-            query = jnp.dot(q_all[here, :], w_even[j], preferred_element_type=jnp.float32)
-            queries[here, :] = (query * q_scale).astype(jnp.bfloat16)
+            top = top_logits(i, block)
+            best = top if best is None else jnp.maximum(best, top)
+        best = jnp.broadcast_to(jnp.max(best, axis=1, keepdims=True), (1, LANES))
         for block in range(n):
-            top_logits(2 * j, block, queries[block * rows : (block + 1) * rows, :])
-        take(j, (2,), near)
+            maxima[block, i : i + 1, rows : rows + LANES] = best
+
+    def side_of(is_far, depth):
+        side = 1 - s // half if is_far else s // half
+        return pl.ds(pl.multiple_of(side * depth, depth), depth)
+
+    close, distant = side_of(False, half * q_rows), side_of(True, half * q_rows)
+
+    def project(weight):
         for block in range(n):
-            here = slice(block * rows, (block + 1) * rows)
-            near_sum[here, :] = jnp.dot(
-                q_all[here, pl.ds(close, depth)], w_odd[j, pl.ds(close, depth), :], preferred_element_type=jnp.float32
-            )
-        take(j, (2,), far)
-        for block in range(n):
-            here = slice(block * rows, (block + 1) * rows)
-            query = near_sum[here, :] + jnp.dot(
-                q_all[here, pl.ds(distant, depth)], w_odd[j, pl.ds(distant, depth), :], preferred_element_type=jnp.float32
-            )
-            queries[here, 0:LANES] = (query * q_scale).astype(jnp.bfloat16)
-        for block in range(n):
-            top_logits(2 * j + 1, block, queries[block * rows : (block + 1) * rows, :])
-        return carry
-
-    lax.fori_loop(0, pairs, head_pair, 0)
-
-    best = jnp.max(maxima[0:own, :], axis=1, keepdims=True)
-    maxima[own : 2 * own, :] = jnp.broadcast_to(best, (own, maxima.shape[1]))
-    shares = []
+            query = jnp.dot(q_all[span(block), :], weight[...], preferred_element_type=jnp.float32)
+            yield block, (query * q_scale).astype(jnp.bfloat16)
+
+    take(KEY, far + near)
+    for block in range(n):
+        key = jnp.dot(kv_all[span(block), :], w_key[...], preferred_element_type=jnp.float32)
+        key = (key * k_scale).astype(jnp.bfloat16)
+        for i in range(own):
+            keys[i, span(block), 0:LANES] = key[:, i * LANES : (i + 1) * LANES]
+    take(ROPE, far + near)
+    for block, query in project(w_pos):
+        q_pos[span(block), :] = query
+    take(GROUP, far + near)
+    for block, query in project(w_group):
+        for i in range(own - 2):
+            q_nope[i, span(block), :] = query[:, i * LANES : (i + 1) * LANES]
+    for i in range(own - 2):
+        head_logits(i)
+    take(SINGLE, far + near)
+    for block, query in project(w_lone.at[0]):
+        q_nope[own - 2, span(block), :] = query
+    head_logits(own - 2)
+    take(FINAL, near)
+    for block in range(n):
+        near_query[span(block), :] = jnp.dot(
+            q_all[span(block), close], w_lone[1, close, :], preferred_element_type=jnp.float32
+        )
+    take(FINAL, far)
+    for block in range(n):
+        query = near_query[span(block), :] + jnp.dot(
+            q_all[span(block), distant], w_lone[1, distant, :], preferred_element_type=jnp.float32
+        )
+        q_nope[own - 1, span(block), :] = (query * q_scale).astype(jnp.bfloat16)
+    head_logits(own - 1)
+
     for k in range(1, n):
         p = flip(s, k)
-        copy = pltpu.make_async_remote_copy(
-            src_ref=maxima.at[:, pl.ds(pl.multiple_of(p * rows, rows), rows)], dst_ref=got.at[s],
-            send_sem=max_send.at[k], recv_sem=max_recv.at[k], device_id=(p, h), device_id_type=MESH)
-        copy.start()
-        shares.append(copy)
-    got[s] = maxima[:, pl.ds(pl.multiple_of(s * rows, rows), rows)]
+        pltpu.make_async_remote_copy(
+            src_ref=maxima.at[p], dst_ref=got.at[s], send_sem=max_send.at[k], recv_sem=max_recv.at[k],
+            device_id=(p, h), device_id_type=MESH).start()
+        drains.append((maxima.at[p], max_send.at[k]))
+    got[s] = maxima[s]
     for ref, sent in drains:
         pltpu.make_async_copy(ref, ref, sent).wait()
-    for k, copy in zip(range(1, n), shares):
-        copy.wait_send()
-        at = got.at[flip(s, k)]
-        pltpu.make_async_copy(at, at, max_recv.at[k]).wait()
+    for k in range(1, n):
+        come = got.at[flip(s, k)]
+        pltpu.make_async_copy(come, come, max_recv.at[k]).wait()
 
 
 def layer(n, m, own, q_lat, kv_lat, rope, segs, w_nope, w_rope, w_kv):
@@ -445,13 +452,15 @@
     tokens = n * rows
     pairs = own // 2
     moves = n * m - 1
-    parts = 3 * pairs + 1
+    parts = len(KINDS)
+    depth = n * w_nope.shape[0]
+    across = (n, own, rows + LANES)
     any_ref = pl.BlockSpec(memory_space=pl.ANY)
     dma = pltpu.SemaphoreType.DMA
     kind = q_lat.dtype
     return pl.pallas_call(
         functools.partial(layer_kernel, n, m, own),
-        out_shape=(pltpu.VMEM((n, 2 * own, rows), jnp.float32),)
+        out_shape=(pltpu.VMEM(across, jnp.float32),)
         + tuple(pltpu.VMEM(w.shape, w.dtype) for w in (w_nope, w_rope, w_kv)),
         in_specs=[any_ref] * 7,
         out_specs=(pl.BlockSpec(memory_space=pltpu.VMEM),) * 4,
@@ -460,17 +469,19 @@
             pltpu.VMEM((tokens, m * kv_lat.shape[1]), kind),
             pltpu.VMEM((n,) + rope.shape, kind),
             pltpu.VMEM((n,) + segs.shape, jnp.int32),
-            pltpu.VMEM((pairs, n * w_nope.shape[0], 2 * LANES), kind),
-            pltpu.VMEM((pairs, n * w_nope.shape[0], LANES), kind),
+            pltpu.VMEM((depth, pairs * LANES), kind),
             pltpu.VMEM((n * w_kv.shape[0], own * LANES), kind),
+            pltpu.VMEM((depth, (own - 2) * LANES), kind),
+            pltpu.VMEM((2, depth, LANES), kind),
             pltpu.VMEM((own, tokens, D_NOPE + LANES), kind),
             pltpu.VMEM((n, (REACH + 1) * rows, rows), jnp.float32),
             pltpu.VMEM((tokens, LANES), jnp.int32),
-            pltpu.VMEM((tokens, 2 * LANES), kind),
+            pltpu.VMEM((tokens, pairs * LANES), kind),
+            pltpu.VMEM((own, tokens, LANES), kind),
             pltpu.VMEM((tokens, LANES), jnp.float32),
-            pltpu.VMEM((2 * own, tokens), jnp.float32),
+            pltpu.VMEM(across, jnp.float32),
             dma((moves,)), dma((n * m,)), dma((moves,)), dma((n * m,)), dma((moves,)), dma((n * m,)),
-            dma((n,)), dma((n,)),
+            dma((moves,)), dma((n * m,)),
             dma((parts * n,)), dma((parts * n,)), dma((n,)), dma((n,)), dma((7 + parts,)),
         ],
         compiler_params=pltpu.CompilerParams(
@@ -482,38 +493,47 @@
 
 def clip_kernel(
     n, own, got, threshold, w_nope, w_rope, w_kv, new_nope, new_rope, new_kv, head_max, row_max,
-    out_nope, out_rope, out_kv, sems,
+    out_nope, out_rope, out_kv, out_head, out_row, sems,
 ):
     limit = threshold[0]
+    rows = row_max.shape[1]
     lane = lax.broadcasted_iota(jnp.int32, (1, LANES), 1)
     tops = jnp.zeros((1, head_max.shape[1]), jnp.float32)
     place = lax.broadcasted_iota(jnp.int32, tops.shape, 1)
     copies = []
 
+    def put(source, target):
+        copy = pltpu.make_async_copy(source, target, sems.at[len(copies)])
+        copy.start()
+        copies.append(copy)
+
     def scaled(source, target, column, factor):
         columns = slice(column * LANES, (column + 1) * LANES)
         target[:, columns] = (source[:, columns].astype(jnp.float32) * factor).astype(target.dtype)
 
     for s in range(n):
-        top = got[s, own : 2 * own, 0:LANES]
+        top = got[s, :, rows : rows + LANES]
         clip = limit / jnp.maximum(top, limit)
         root = jnp.sqrt(clip)
         for i in range(own):
-            head = s * own + i
-            scaled(w_nope, out_nope, head, root[i : i + 1])
-            scaled(w_kv, out_kv, head, root[i : i + 1])
-            tops = jnp.where(place == head, top[i : i + 1, 0 : tops.shape[1]], tops)
+            scaled(w_nope, out_nope, s * own + i, root[i : i + 1])
+        for i in range(own):
+            scaled(w_kv, out_kv, s * own + i, root[i : i + 1])
         for j in range(own // 2):
             factor = jnp.where(lane < D_ROPE, clip[2 * j : 2 * j + 1], clip[2 * j + 1 : 2 * j + 2])
             scaled(w_rope, out_rope, s * own // 2 + j, factor)
-        for i, (source, target) in enumerate(((out_nope, new_nope), (out_rope, new_rope), (out_kv, new_kv))):
+        for source, target in ((out_nope, new_nope), (out_rope, new_rope), (out_kv, new_kv)):
             width = source.shape[1] // n
             at = pl.ds(s * width, width)
-            copy = pltpu.make_async_copy(source.at[:, at], target.at[:, at], sems.at[3 * s + i])
-            copy.start()
-            copies.append(copy)
-        row_max[s * own : (s + 1) * own, :] = got[s, 0:own, :]
-    head_max[...] = tops
+            put(source.at[:, at], target.at[:, at])
+        if s == 0:
+            for p in range(n):
+                out_row[p * own : (p + 1) * own, :] = got[p, :, 0:rows]
+                for i in range(own):
+                    tops = jnp.where(place == p * own + i, got[p, i : i + 1, rows : rows + tops.shape[1]], tops)
+            out_head[...] = tops
+            put(out_row, row_max)
+            put(out_head, head_max)
     for copy in copies:
         copy.wait()
 
@@ -521,15 +541,17 @@
 def clip_weights(n, own, got, threshold, w_nope, w_rope, w_kv):
     weights = (w_nope, w_rope, w_kv)
     heads = n * own
+    rows = got.shape[2] - LANES
     in_vmem = pl.BlockSpec(memory_space=pltpu.VMEM)
-    any_ref = pl.BlockSpec(memory_space=pl.ANY)
     return pl.pallas_call(
         functools.partial(clip_kernel, n, own),
         out_shape=tuple(jax.ShapeDtypeStruct(w.shape, w.dtype) for w in weights)
-        + (jax.ShapeDtypeStruct((1, heads), jnp.float32), jax.ShapeDtypeStruct((heads, got.shape[2]), jnp.float32)),
+        + (jax.ShapeDtypeStruct((1, heads), jnp.float32), jax.ShapeDtypeStruct((heads, rows), jnp.float32)),
         in_specs=[in_vmem, pl.BlockSpec(memory_space=pltpu.SMEM)] + [in_vmem] * 3,
-        out_specs=(any_ref,) * 3 + (in_vmem,) * 2,
-        scratch_shapes=[pltpu.VMEM(w.shape, w.dtype) for w in weights] + [pltpu.SemaphoreType.DMA((3 * n,))],
+        out_specs=(pl.BlockSpec(memory_space=pl.ANY),) * 5,
+        scratch_shapes=[pltpu.VMEM(w.shape, w.dtype) for w in weights]
+        + [pltpu.VMEM((1, heads), jnp.float32), pltpu.VMEM((heads, rows), jnp.float32)]
+        + [pltpu.SemaphoreType.DMA((3 * n + 2,))],
         compiler_params=pltpu.CompilerParams(vmem_limit_bytes=16 * 1024 * 1024),
         name="clip_weights",
     )(

time: 94.7 us -> 93.6 us (0.988)
  Pallas kernels: 93.2 us -> 92.1 us
where the time goes in v4:
time: 93.6 us; the launch traced here: 93.4 us
  Pallas kernels  92.1 us (98%)
  between operations  1.29 us (1%)
    pallas_call x1, Pallas kernels, layer(): pl.pallas_call(functools.partial(layer_kernel, n, m, own), out_shape=(plt...  90.2 us

profile of v4, /device:TPU:0, one launch (start us, length us, event | category | flops | bytes accessed | tf_op | source)
XLA Modules:
  0.0 93.4 jit_solution(17475488716206032633)
XLA Ops:
  1.3 90.2 %layer.1 = (f32[8,4,384]{2,1,0:T(4,128)S(1)}, bf16[192,4096]{1,0:T(8,128)(2,1)S(1)}, bf16[192,2048]{1,0:T(8,128)(2,1)S(1)}, bf16[64,4096]{1,0:T(8,128)(2,1)S(1)}) custom-call(bf16[256,384]{1,0:T(8,128)(2,1)} %q_lat.1, bf16[256,128]{1,0:T(8,128)(2,1)} %kv_lat.1, bf16[64,256]{1,0:T(8,128)(2,1)} %bitcast.4, s32[1,256]{1,0:T(1,128)} %bitcast.5, ...), custom_call_target="tpu_custom_call" | custom-call | tf_op jit(solution)/shard_map/layer/pallas_call | solution.py:461
  91.5 1.9 %clip_weights.1 = (bf16[192,4096]{1,0:T(8,128)(2,1)}, bf16[192,2048]{1,0:T(8,128)(2,1)}, bf16[64,4096]{1,0:T(8,128)(2,1)}, f32[1,32]{1,0:T(1,128)}, f32[32,256]{1,0:T(8,128)}) custom-call(f32[8,4,384]{2,1,0:T(4,128)S(1)} %get-tuple-element.14.got, f32[1]{0:T(128)S(6)} %copy.13.threshold, bf16[192,4096]{1,0:T(8,128)(2,1)S(1)} %get-tuple-element.15.w_nope, ...), custom_call_target="tpu_custom_call" | custom-call | tf_op jit(solution)/shard_map/clip_weights/pallas_call | solution.py:546

commit v5 on v4

--- a/solution.py
+++ b/solution.py
@@ -189,7 +189,7 @@
     n, m, own, q_lat, kv_lat, rope, segs, w_nope, w_rope, w_kv,
     got, held_nope, held_rope, held_kv,
     q_all, kv_all, rope_all, segs_all, w_pos, w_key, w_group, w_lone, keys, caps, seg_cols, q_pos, q_nope, near_query, maxima,
-    q_send, q_recv, kv_send, kv_recv, rope_send, rope_recv, seg_send, seg_recv, w_send, w_recv, max_send, max_recv, local,
+    q_send, q_recv, kv_send, kv_recv, rope_send, rope_recv, seg_send, seg_recv, w_send, w_recv, max_send, max_recv, local, known,
 ):
     s = lax.axis_index("seq")
     h = lax.axis_index("head")
@@ -203,8 +203,8 @@
     last = len([1 for axis, _ in routes if axis == "seq"])
 
     barrier = pltpu.get_barrier_semaphore()
-    for k in range(1, n):
-        pl.semaphore_signal(barrier, inc=1, device_id=(flip(s, k), h), device_id_type=MESH)
+    for stride in halvings(n):
+        pl.semaphore_signal(barrier, inc=1, device_id=(other(s, stride), h), device_id_type=MESH)
     for stride in halvings(m):
         pl.semaphore_signal(barrier, inc=1, device_id=(s, other(h, stride)), device_id_type=MESH)
 
@@ -255,7 +255,7 @@
     ]
     for copy in keeps:
         copy.start()
-    pl.semaphore_wait(barrier, n - 1 + len(halvings(m)))
+    pl.semaphore_wait(barrier, len(routes))
     for copy in loads:
         copy.wait()
 
@@ -305,6 +305,9 @@
 
     for route in routes:
         push(0, 0, route)
+    for i, stride in enumerate(reversed(halvings(n)[:-1])):
+        pl.semaphore_signal(known.at[i], inc=1, device_id=(other(s, stride), h), device_id_type=MESH)
+        pl.semaphore_wait(known.at[i], 1)
     for k in far:
         weights(ROPE, k)
     order = sorted(range(1, n), key=lambda k: (bin(k).count("1"), k & 1 == 1 and bin(k).count("1") > 1, k))
@@ -483,6 +486,7 @@
             dma((moves,)), dma((n * m,)), dma((moves,)), dma((n * m,)), dma((moves,)), dma((n * m,)),
             dma((moves,)), dma((n * m,)),
             dma((parts * n,)), dma((parts * n,)), dma((n,)), dma((n,)), dma((7 + parts,)),
+            pltpu.SemaphoreType.REGULAR((n.bit_length(),)),
         ],
         compiler_params=pltpu.CompilerParams(
             collective_id=0, has_side_effects=True, vmem_limit_bytes=60 * 1024 * 1024

time: 93.6 us -> 92.4 us (0.987)
  Pallas kernels: 92.1 us -> 91 us
    pallas_call x1, Pallas kernels: 90.2 us -> 89.1 us  [layer(): pl.pallas_call(functools.partial(layer_kernel, n, m, own), out_shape=(plt...]
where the time goes in v5:
time: 92.4 us; the launch traced here: 92.2 us
  Pallas kernels  91 us (98%)
  between operations  1.29 us (1%)
    pallas_call x1, Pallas kernels, layer(): pl.pallas_call(functools.partial(layer_kernel, n, m, own), out_shape=(plt...  89.1 us
    pallas_call x1, Pallas kernels, clip_weights(): pl.pallas_call(functools.partial(clip_kernel, n, own), out_shape=tuple((j...  1.87 us

profile of v5, /device:TPU:0, one launch (start us, length us, event | category | flops | bytes accessed | tf_op | source)
XLA Modules:
  0.0 92.2 jit_solution(4981414758522480979)
XLA Ops:
  1.3 89.1 %layer.1 = (f32[8,4,384]{2,1,0:T(4,128)S(1)}, bf16[192,4096]{1,0:T(8,128)(2,1)S(1)}, bf16[192,2048]{1,0:T(8,128)(2,1)S(1)}, bf16[64,4096]{1,0:T(8,128)(2,1)S(1)}) custom-call(bf16[256,384]{1,0:T(8,128)(2,1)} %q_lat.1, bf16[256,128]{1,0:T(8,128)(2,1)} %kv_lat.1, bf16[64,256]{1,0:T(8,128)(2,1)} %bitcast.4, s32[1,256]{1,0:T(1,128)} %bitcast.5, ...), custom_call_target="tpu_custom_call" | custom-call | tf_op jit(solution)/shard_map/layer/pallas_call | solution.py:464
  90.4 1.9 %clip_weights.1 = (bf16[192,4096]{1,0:T(8,128)(2,1)}, bf16[192,2048]{1,0:T(8,128)(2,1)}, bf16[64,4096]{1,0:T(8,128)(2,1)}, f32[1,32]{1,0:T(1,128)}, f32[32,256]{1,0:T(8,128)}) custom-call(f32[8,4,384]{2,1,0:T(4,128)S(1)} %get-tuple-element.14.got, f32[1]{0:T(128)S(6)} %copy.13.threshold, bf16[192,4096]{1,0:T(8,128)(2,1)S(1)} %get-tuple-element.15.w_nope, ...), custom_call_target="tpu_custom_call" | custom-call | tf_op jit(solution)/shard_map/clip_weights/pallas_call | solution.py:550
